TPU v7x, 128 devices: a whole 4x4x4 slice. The times are simulated.
128 devices in a mesh: dp: 1, tp: 128 (over z, y, x, core).
Axes of the slice: x: 4, y: 4, z: 4, core: 2. Of those that a mesh axis runs over, the one named last changes fastest.
Arguments:
- hidden: bfloat16 [4096, 1152], P(('dp', 'tp'))
- w_head: bfloat16 [1152, 262144], P(None, 'tp')
- labels: int32 [4096], P(('dp', 'tp'))
Outputs:
- output 1: float32 [1], P('dp')
- output 2: bfloat16 [4096, 1152], P(('dp', 'tp'))
- output 3: bfloat16 [1152, 262144], P('dp', 'tp')
All inputs are finite; a program needn't handle non-finite values.
Results may differ from a plain program's by a relative error of at most 0.001.
Values are sent between devices in bfloat16 or wider.
A program may use at most 1 GiB of HBM per device.

v0:
```python
import jax
import jax.numpy as jnp
from jax import lax
from jax.sharding import PartitionSpec as P


def solution(mesh):
    group_size = mesh.shape["tp"]

    def local_step(hid_loc, w_loc, lab_loc):
        inv_tokens = 1.0 / (hid_loc.shape[0] * group_size)
        vocab_loc = w_loc.shape[1]
        hid_all = lax.all_gather(hid_loc, "tp", axis=0, tiled=True)
        lab_all = lax.all_gather(lab_loc, "tp", axis=0, tiled=True)
        logits = jnp.dot(hid_all, w_loc, preferred_element_type=jnp.float32)
        glob_max = lax.pmax(jnp.max(logits, axis=1), "tp")
        shifted = jnp.exp(logits - glob_max[:, None])
        local_ids = lab_all - lax.axis_index("tp") * vocab_loc
        is_label = jnp.arange(vocab_loc, dtype=jnp.int32) == local_ids[:, None]
        local_stats = jnp.stack([jnp.sum(shifted, axis=1), jnp.sum(jnp.where(is_label, logits, 0.0), axis=1)])
        stat_sums = lax.psum(local_stats, "tp")
        row_sum = stat_sums[0]
        token_loss = glob_max + jnp.log(row_sum) - stat_sums[1]
        mean_loss = (jnp.sum(token_loss) * inv_tokens).reshape(1)
        prob_rows = shifted / row_sum[:, None]
        grad_out = (jnp.where(is_label, prob_rows - 1.0, prob_rows) * inv_tokens).astype(jnp.bfloat16)
        d_head = lax.dot_general(hid_all, grad_out, (((0,), (0,)), ((), ())), preferred_element_type=jnp.float32)
        dx_part = lax.dot_general(grad_out, w_loc, (((1,), (1,)), ((), ())), preferred_element_type=jnp.float32)
        d_hidden = lax.psum_scatter(dx_part, "tp", scatter_dimension=0, tiled=True)
        return mean_loss, d_hidden.astype(jnp.bfloat16), d_head.astype(jnp.bfloat16)

    return jax.shard_map(
        local_step,
        mesh=mesh,
        in_specs=(P(("dp", "tp"), None), P(None, "tp"), P(("dp", "tp"))),
        out_specs=(P("dp"), P(("dp", "tp"), None), P("dp", "tp")),
        check_vma=False,
    )
```

profile of v0, /device:TPU:1, one launch (start us, length us, event | category | flops | bytes accessed | tf_op | source)
XLA Modules:
  0.0 548.7 jit_solution(5699444816640139430)
XLA Ops:
  7.2 0.0 all-gather.2.cloned.1.call-start
  7.2 0.7 all-gather.2.cloned.1.call-update
  7.9 0.0 reduce-scatter.2.cloned.1.call-start
  8.0 0.9 dynamic-update-slice
  8.8 69.6 %all-reduce = s32[4096]{0:T(1024)S(1)} all-reduce(s32[4096]{0:T(1024)S(1)} %dynamic-update-slice), channel_id=1, replica_groups=mesh['dp'=1,'tp'=128] {'tp'}, use_global_device_ids=true, to_apply=%add | all-reduce | flops 4096 | bytes 32768
  78.4 7.0 %all-gather.2.cloned.1.call-done = bf16[4096,1152]{1,0:T(8,128)(2,1)} async-done(((bf16[32,1152]{1,0:T(8,128)(2,1)}), bf16[4096,1152]{1,0:T(8,128)(2,1)}) %all-gather.2.cloned.1.call-update) | async-done | bytes 9437200 | tf_op jit(solution)/shard_map/all_gather | solution.py:13
  85.4 29.0 %fusion.5 = (f32[4096]{0:T(1024)S(1)}, f32[4096,2048]{0,1:T(8,128)}) fusion(bf16[4096,1152]{1,0:T(8,128)(2,1)} %all-gather.2.cloned.1.call-done, bf16[1152,2048]{1,0:T(8,128)(2,1)} %param.4), kind=kOutput, calls=%fused_computation.13 | convolution fusion | flops 19335737344 | bytes 47726592 | tf_op jit(solution)/shard_map/dot_general | solution.py:15
  114.4 63.0 %pmax.7 = f32[4096]{0:T(1024)S(1)} all-reduce(f32[4096]{0:T(1024)S(1)} %get-tuple-element.10), channel_id=1, replica_groups=mesh['dp'=1,'tp'=128] {'tp'}, use_global_device_ids=true, to_apply=%region_1.0 | all-reduce | flops 4096 | bytes 32768 | tf_op jit(solution)/shard_map/pmax | solution.py:16
  177.5 15.2 %fusion.2 = (f32[4096]{0:T(1024)S(1)}, f32[4096]{0:T(1024)S(1)}) fusion(f32[4096,2048]{0,1:T(8,128)} %get-tuple-element.11, f32[4096]{0:T(1024)S(1)} %pmax.7, s32[4096]{0:T(1024)S(1)} %broadcast_subtract_fusion), kind=kLoop, calls=%fused_computation.6 | loop fusion | flops 41934848 | bytes 33619968 | tf_op jit(solution)/shard_map/reduce_sum | solution.py:20
  192.7 63.2 %psum.7 = f32[2,4096]{1,0:T(2,128)S(1)} all-reduce(f32[2,4096]{1,0:T(2,128)S(1)} %pad_maximum_fusion), channel_id=1, replica_groups=mesh['dp'=1,'tp'=128] {'tp'}, use_global_device_ids=true, to_apply=%region_4.5 | all-reduce | flops 8192 | bytes 65536 | tf_op jit(solution)/shard_map/psum | solution.py:21
  256.0 15.8 %fusion.1 = bf16[4096,2048]{0,1:T(8,128)(2,1)S(1)} fusion(f32[4096,2048]{0,1:T(8,128)} %get-tuple-element.11, f32[4096]{0:T(1024)S(1)} %bitcast.13, s32[4096]{0:T(1024)S(1)} %broadcast_subtract_fusion, f32[4096]{0:T(1024)S(1)} %pmax.7), kind=kLoop, calls=%fused_computation.2 | loop fusion | flops 58720256 | bytes 50380800 | tf_op jit(solution)/shard_map/convert_element_type | solution.py:26
  271.8 0.0 copy-start
  271.8 5.8 %copy-done = bf16[4096,2048]{0,1:T(8,128)(2,1)} copy-done((bf16[4096,2048]{0,1:T(8,128)(2,1)}, bf16[4096,2048]{0,1:T(8,128)(2,1)S(1)}, u32[]{:S(2)}) %copy-start) | copy-done | bytes 16777240
  277.6 30.2 %fusion.6 = f32[4096,1152]{1,0:T(8,128)} fusion(bf16[4096,2048]{0,1:T(8,128)(2,1)S(1)} %fusion.1, bf16[1152,2048]{1,0:T(8,128)(2,1)} %param.4), kind=kOutput, calls=%fused_computation.14 | convolution fusion | flops 19327352832 | bytes 40370176 | tf_op jit(solution)/shard_map/dot_general | solution.py:28
  307.8 0.0 reduce-scatter.2.cloned.1.call-update
  307.8 28.3 %fusion.3 = bf16[1152,2048]{0,1:T(8,128)(2,1)} fusion(bf16[4096,2048]{0,1:T(8,128)(2,1)} %copy-done, bf16[4096,1152]{1,0:T(8,128)(2,1)} %all-gather.2.cloned.1.call-done), kind=kOutput, calls=%fused_computation.8 | convolution fusion | flops 19329712128 | bytes 30932992 | tf_op jit(solution)/shard_map/dot_general | solution.py:27
  336.1 6.6 %copy.6 = bf16[1152,2048]{1,0:T(8,128)(2,1)} copy(bf16[1152,2048]{0,1:T(8,128)(2,1)} %fusion.3) | data formatting | bytes 9437184
  342.7 0.6 subtract_reduce_fusion
  344.0 195.2 %reduce-scatter.2.cloned.1.call-done = f32[32,1152]{1,0:T(8,128)} async-done(((f32[4096,1152]{1,0:T(8,128)}), f32[32,1152]{1,0:T(8,128)}) %reduce-scatter.2.cloned.1.call-update) | async-done | bytes 147472 | tf_op jit(solution)/shard_map/reduce_scatter | solution.py:29
  539.2 1.6 convert_element_type.13
  (4 shorter events, 0.1 us)
Async XLA Ops:
  7.2 78.3 %all-gather.2.cloned.1.call-start = ((), (), s32[]{:S(2)}) async-start(), calls=%async_computation.1 | async-start | bytes 9510912 | tf_op jit(solution)/shard_map/all_gather | solution.py:13
  7.9 531.3 %reduce-scatter.2.cloned.1.call-start = ((), (), s32[]{:S(2)}) async-start(), calls=%async_computation.2 | async-start | bytes 19021824 | tf_op jit(solution)/shard_map/reduce_scatter | solution.py:29
  271.8 5.8 %copy-start = (bf16[4096,2048]{0,1:T(8,128)(2,1)}, bf16[4096,2048]{0,1:T(8,128)(2,1)S(1)}, u32[]{:S(2)}) copy-start(bf16[4096,2048]{0,1:T(8,128)(2,1)S(1)} %fusion.1) | copy-start | bytes 50331652
Sparse Core Ops, SparseCore 0:
  11.0 74.4 all-gather.1
  307.9 231.2 reduce-scatter.1
where the time goes:
time: 551 us; the launch traced here: 549 us
  waiting for transfers between devices  203 us (37%)
  blocking collectives  196 us (36%)
  matrix products  87.5 us (16%)
  other arithmetic  33.2 us (6%)
  between operations  15.9 us (3%)
  local copies, waits for them, and re-layouts  13.3 us (2%)
    reduce_scatter x1, waiting for transfers between devices, local_step(): d_hidden = lax.psum_scatter(dx_part, 'tp', scatter_dimension=0, tiled=True)  195 us
    unnamed x1, blocking collectives  69.6 us
    psum x1, blocking collectives, local_step(): stat_sums = lax.psum(local_stats, 'tp')  63.2 us
    pmax x1, blocking collectives, local_step(): glob_max = lax.pmax(jnp.max(logits, axis=1), 'tp')  63 us
    dot_general x1, matrix products, local_step(): lax.dot_general(grad_out, w_loc, (((1,), (1,)), ((), ())), preferred_elem...  30.2 us
    dot_general x1, matrix products, local_step(): logits = jnp.dot(hid_all, w_loc, preferred_element_type=jnp.float32)  29 us
    dot_general x1, matrix products, local_step(): lax.dot_general(hid_all, grad_out, (((0,), (0,)), ((), ())), preferred_el...  28.3 us
    convert_element_type x1, other arithmetic, local_step(): (jnp.where(is_label, prob_rows - 1.0, prob_rows) * inv_tokens).astype(jnp...  15.8 us
  transfers between devices with their start and end apart: 2, of which 2 were waited for; matrix products, arithmetic and copies ran while one was open for 7% of the time, Pallas kernels for 0%

commit v1 on v0

v1 whole, which is shorter than its diff:
```python
import functools

import jax
import jax.numpy as jnp
from jax import lax
from jax.experimental import pallas as pl
from jax.experimental.pallas import tpu as pltpu
from jax.sharding import PartitionSpec as P

MESH = pl.DeviceIdType.MESH
F32 = jnp.float32
BF16 = jnp.bfloat16

SIDE = 4
STRIDES = (32, 8, 2)
ORDERS = ((2, 1, 0), (1, 0, 2), (0, 2, 1))
SLABS = 2
ROWS = 16
BLOCK = 256
HID = 1152
COLOUR = HID // 3
HALF = 2048
TOKENS = 4096
INV = 1.0 / TOKENS
LANES = 128


def body(x_hbm, w_hbm, lab_hbm,
         loss_ref, dhid_ref, dhead_hbm, p_hbm, hrecv_hbm,
         x_ref, w_ref, g_ref, dx_ref, buf_ref, r1_ref, r2_ref, r3_ref,
         labrow_ref, lab_ref, m_ref, s_ref, t_ref, scale_ref, srow_ref, st_ref, fin_ref, lossx_ref,
         ag_send, ag_recv, lab_send, lab_recv, w_send, w_recv, st_send, st_recv, rs_send, rs_recv,
         hd_send, hd_recv, ls_send, ls_recv, in_sem, p_sem, g_sem, h_sem, out_sem):
    me = lax.axis_index("tp")
    core = lax.rem(me, 2)
    chip = lax.div(me, 2)
    coords = (lax.div(chip, 16), lax.rem(lax.div(chip, 4), 4), lax.rem(chip, 4))
    partner = me + 1 - 2 * core

    def ring(axis, d):
        return lax.rem(coords[axis] + d, SIDE)

    def rank(axis, d):
        return me + (ring(axis, d) - coords[axis]) * STRIDES[axis]

    def remote(src, dst, send, recv, target):
        return pltpu.make_async_remote_copy(src_ref=src, dst_ref=dst, send_sem=send, recv_sem=recv,
                                            device_id={"tp": target}, device_id_type=MESH)

    def cols(c):
        return pl.ds(COLOUR * c, COLOUR)

    own = []
    for s in range(SLABS):
        own.append(pltpu.make_async_copy(x_hbm.at[pl.ds(ROWS * s, ROWS)],
                                         x_ref.at[(s,) + coords], in_sem.at[s]))
    own.append(pltpu.make_async_copy(lab_hbm, labrow_ref.at[coords], in_sem.at[2]))
    w_own = pltpu.make_async_copy(w_hbm, w_ref.at[core], in_sem.at[3])
    for copy in own:
        copy.start()
    w_own.start()

    barrier = pltpu.get_barrier_semaphore()
    peers = [partner] + [rank(a, d) for a in range(3) for d in (1, 2, 3)]
    for peer in peers:
        pl.semaphore_signal(barrier, inc=1, device_id={"tp": peer}, device_id_type=MESH)
    pl.semaphore_wait(barrier, len(peers))

    def ag_copy(s, phase, c, d):
        order = ORDERS[c]
        idx = list(coords)
        for a in order[:phase]:
            idx[a] = slice(None)
        view = x_ref.at[(s,) + tuple(idx) + (slice(None), cols(c))]
        return remote(view, view, ag_send.at[s, phase, c, d - 1], ag_recv.at[s, phase, c, d - 1],
                      rank(order[phase], d))

    def ag_start(s, phase):
        for d in (2, 1, 3):
            for c in range(3):
                ag_copy(s, phase, c, d).start()

    def ag_wait(s, phase):
        for d in (1, 2, 3):
            for c in range(3):
                ag_copy(s, phase, c, d).wait_recv()

    def lab_copy(phase, d):
        order = ORDERS[0]
        idx = list(coords)
        for a in order[:phase]:
            idx[a] = slice(None)
        view = labrow_ref.at[tuple(idx)]
        return remote(view, view, lab_send.at[phase, d - 1], lab_recv.at[phase, d - 1], rank(order[phase], d))

    def lab_start(phase):
        for d in (1, 2, 3):
            lab_copy(phase, d).start()

    def lab_wait(phase):
        for d in (1, 2, 3):
            lab_copy(phase, d).wait_recv()

    for copy in own:
        copy.wait()
    lab_start(0)
    ag_start(0, 0)
    ag_start(1, 0)
    w_copy = remote(w_hbm, w_ref.at[core], w_send, w_recv, partner)
    w_copy.start()
    lab_wait(0)
    lab_start(1)
    ag_wait(0, 0)
    ag_start(0, 1)
    ag_wait(1, 0)
    ag_start(1, 1)
    lab_wait(1)
    lab_start(2)
    ag_wait(0, 1)
    ag_start(0, 2)
    ag_wait(1, 1)
    ag_start(1, 2)
    lab_wait(2)

    lane16 = lax.broadcasted_iota(jnp.int32, (ROWS, LANES), 1)
    row16 = lax.broadcasted_iota(jnp.int32, (ROWS, LANES), 0)
    first_col = chip * (2 * HALF)

    def spread(k, carry):
        kz, ky, kx = lax.div(k, 16), lax.rem(lax.div(k, 4), 4), lax.rem(k, 4)
        row = jnp.broadcast_to(labrow_ref[kz, ky, kx], (ROWS, LANES)).astype(F32)
        for s in range(SLABS):
            col = jnp.sum(jnp.where(lane16 == row16 + ROWS * s, row, 0.0), axis=1, keepdims=True)
            lab_ref[s, k] = jnp.broadcast_to(col, (ROWS, LANES)).astype(jnp.int32) - first_col - lane16
        return carry

    lax.fori_loop(0, 64, spread, 0, unroll=4)

    def p_copy(n, slot):
        return pltpu.make_async_copy(buf_ref.at[slot, pl.ds(0, 1024)], p_hbm.at[n], p_sem.at[slot])

    def g_load(n, slot):
        return pltpu.make_async_copy(p_hbm.at[n], buf_ref.at[slot, pl.ds(0, 1024)], g_sem.at[slot])

    def st_copy(s, axis, d):
        view = st_ref.at[s, axis, coords[axis]]
        return remote(view, view, st_send.at[s, axis, d - 1], st_recv.at[s, axis, d - 1], rank(axis, d))

    def st_start(s, axis):
        for d in (2, 1, 3):
            st_copy(s, axis, d).start()

    def st_merge(s, axis):
        for d in (1, 2, 3):
            st_copy(s, axis, d).wait_recv()
        top = st_ref[s, axis, 0, 0]
        for i in range(1, SIDE):
            top = jnp.maximum(top, st_ref[s, axis, i, 0])
        total = jnp.zeros_like(top)
        target = jnp.zeros_like(top)
        for i in range(SIDE):
            total += st_ref[s, axis, i, 1] * jnp.exp(st_ref[s, axis, i, 0] - top)
            target += st_ref[s, axis, i, 2]
        if axis < 2:
            here = coords[axis + 1]
            st_ref[s, axis + 1, here, 0] = top
            st_ref[s, axis + 1, here, 1] = total
            st_ref[s, axis + 1, here, 2] = target
            st_start(s, axis + 1)
        else:
            fin_ref[s, 0] = top
            fin_ref[s, 1] = INV / total
            fin_ref[s, 2] = top + jnp.log(total) - target

    def logits_block(s, b):
        n = s * SIDE + b
        slot = lax.rem(n, 2)

        @pl.when(n >= 2)
        def _():
            p_copy(n - 2, slot).wait()

        xb = x_ref[s, b].reshape(BLOCK, HID)
        for q in range(4):
            buf_ref[slot, pl.ds(q * BLOCK, BLOCK), :] = jnp.dot(
                xb, w_ref[q // 2, :, (q % 2) * 1024:(q % 2 + 1) * 1024], preferred_element_type=F32)

        def rows(i, carry):
            r0 = pl.multiple_of(i * 8, 8)
            lab = lab_ref[s, b * 16 + lax.div(i, 2), pl.ds(pl.multiple_of(lax.rem(i, 2) * 8, 8), 8), :]
            z = [buf_ref[slot, pl.ds(pl.multiple_of(q * BLOCK + r0, 8), 8), l * LANES:(l + 1) * LANES]
                 for q in range(4) for l in range(8)]
            tops = z
            while len(tops) > 1:
                tops = [jnp.maximum(tops[k], tops[k + 1]) for k in range(0, len(tops), 2)]
            top = tops[0]
            sums = [jnp.zeros((8, LANES), F32) for _ in range(2)]
            tgt = [jnp.zeros((8, LANES), F32) for _ in range(2)]
            for k in range(32):
                p = jnp.exp(z[k] - top)
                q, l = k // 8, k % 8
                buf_ref[slot, pl.ds(pl.multiple_of(q * BLOCK + r0, 8), 8), l * LANES:(l + 1) * LANES] = p
                sums[k % 2] += p
                tgt[k % 2] = jnp.where(lab == k * LANES, z[k], tgt[k % 2])
            m_ref[s, pl.ds(pl.multiple_of(b * BLOCK + r0, 8), 8), :] = top
            s_ref[pl.ds(r0, 8), :] = sums[0] + sums[1]
            t_ref[pl.ds(r0, 8), :] = tgt[0] + tgt[1]
            return carry

        lax.fori_loop(0, BLOCK // 8, rows, 0, unroll=2)
        p_copy(n, slot).start()
        for i in range(2):
            m_t = m_ref[s, pl.ds(pl.multiple_of(b * BLOCK + i * LANES, LANES), LANES), :].T
            s_t = s_ref[i * LANES:(i + 1) * LANES, :].T
            t_t = t_ref[i * LANES:(i + 1) * LANES, :].T
            top = jnp.max(m_t, axis=0, keepdims=True)
            at = pl.ds(b * 2 + i, 1)
            srow_ref[0, at, :] = top
            srow_ref[1, at, :] = jnp.sum(s_t * jnp.exp(m_t - top), axis=0, keepdims=True)
            srow_ref[2, at, :] = jnp.sum(t_t, axis=0, keepdims=True)

    def st_begin(s):
        for k in range(3):
            st_ref[s, 0, coords[0], k] = srow_ref[k]
        st_start(s, 0)

    def rs_copy(s, phase, c, d):
        order = ORDERS[c]
        idx = [slice(None)] * 3
        for a in order[:phase]:
            idx[a] = coords[a]
        idx[order[phase]] = ring(order[phase], d)
        land = (r1_ref, r2_ref, r3_ref)[phase]
        return remote(dx_ref.at[(s,) + tuple(idx) + (slice(None), cols(c))], land.at[s, c, d - 1],
                      rs_send.at[s, phase, c, d - 1], rs_recv.at[s, phase, c, d - 1], rank(order[phase], d))

    def rs_start(s, phase):
        for d in (2, 1, 3):
            for c in range(3):
                rs_copy(s, phase, c, d).start()

    def rs_add(s, phase):
        for c in range(3):
            for d in (1, 2, 3):
                rs_copy(s, phase, c, d).wait_recv()
            order = ORDERS[c]
            sl = slice(c * COLOUR, (c + 1) * COLOUR)
            idx = [None] * 3
            for a in order[:phase + 1]:
                idx[a] = coords[a]
            free = [a for a in range(3) if idx[a] is None]
            if phase == 0:
                def add(i, carry):
                    for j in range(SIDE):
                        at = list(idx)
                        at[free[0]], at[free[1]] = i, j
                        at = (s,) + tuple(at)
                        dx_ref[at + (slice(None), sl)] = (
                            (dx_ref[at + (slice(None), sl)] + r1_ref[s, c, 0, i, j])
                            + (r1_ref[s, c, 1, i, j] + r1_ref[s, c, 2, i, j]))
                    return carry
                lax.fori_loop(0, SIDE, add, 0)
            elif phase == 1:
                def add(i, carry):
                    at = list(idx)
                    at[free[0]] = i
                    at = (s,) + tuple(at)
                    dx_ref[at + (slice(None), sl)] = (
                        (dx_ref[at + (slice(None), sl)] + r2_ref[s, c, 0, i])
                        + (r2_ref[s, c, 1, i] + r2_ref[s, c, 2, i]))
                    return carry
                lax.fori_loop(0, SIDE, add, 0)
            else:
                total = ((dx_ref[(s,) + tuple(idx) + (slice(None), sl)] + r3_ref[s, c, 0])
                         + (r3_ref[s, c, 1] + r3_ref[s, c, 2]))
                dhid_ref[s * ROWS:(s + 1) * ROWS, sl] = total.astype(BF16)
        if phase < 2:
            rs_start(s, phase + 1)

    def grad_block(s, b):
        n = s * SIDE + b
        slot = lax.rem(n, 2)

        @pl.when(n < 2 * SIDE - 1)
        def _():
            g_load(n + 1, 1 - slot).start()

        for i in range(2):
            at = pl.ds(b * 2 + i, 1)
            top = jnp.broadcast_to(fin_ref[s, 0, at, :], (LANES, LANES)).T
            inv = jnp.broadcast_to(fin_ref[s, 1, at, :], (LANES, LANES)).T
            m = m_ref[s, pl.ds(pl.multiple_of(b * BLOCK + i * LANES, LANES), LANES), :]
            scale_ref[i * LANES:(i + 1) * LANES, :] = jnp.exp(m - top) * inv
        g_load(n, slot).wait()

        def rows(i, carry):
            r0 = pl.multiple_of(i * ROWS, ROWS)
            lab = lab_ref[s, b * 16 + i]
            scale = scale_ref[pl.ds(r0, ROWS), :]
            out_row = pl.multiple_of(n * BLOCK + r0, ROWS)
            for k in range(32):
                q, l = k // 8, k % 8
                p = buf_ref[slot, pl.ds(pl.multiple_of(q * BLOCK + r0, 8), ROWS), l * LANES:(l + 1) * LANES]
                g = p * scale - jnp.where(lab == k * LANES, INV, 0.0)
                g_ref[k // 16, pl.ds(out_row, ROWS), (k % 16) * LANES:(k % 16 + 1) * LANES] = g.astype(BF16)
            return carry

        lax.fori_loop(0, BLOCK // ROWS, rows, 0, unroll=2)
        at = pl.ds(pl.multiple_of(n * BLOCK, BLOCK), BLOCK)
        nt = (((1,), (1,)), ((), ()))
        dx = (lax.dot_general(g_ref[0, at, :], w_ref[0], nt, preferred_element_type=F32)
              + lax.dot_general(g_ref[1, at, :], w_ref[1], nt, preferred_element_type=F32))
        dx_ref[s, b] = dx.reshape(SIDE, SIDE, ROWS, HID)

    w_own.wait()
    w_copy.wait_recv()
    ag_wait(0, 2)

    def logits_first(b, carry):
        logits_block(0, b)
        return carry

    lax.fori_loop(0, SIDE, logits_first, 0)
    st_begin(0)
    ag_wait(1, 2)

    def logits_second(b, carry):
        logits_block(1, b)
        for axis in range(3):
            pl.when(b == axis)(functools.partial(st_merge, 0, axis))
        return carry

    lax.fori_loop(0, SIDE, logits_second, 0)
    st_begin(1)
    p_copy(6, 0).wait()
    p_copy(7, 1).wait()
    g_load(0, 0).start()

    def grad_first(b, carry):
        grad_block(0, b)
        for axis in range(3):
            pl.when(b == axis)(functools.partial(st_merge, 1, axis))
        return carry

    lax.fori_loop(0, SIDE, grad_first, 0)
    rs_start(0, 0)

    lossx_ref[core] = fin_ref[0, 2] + fin_ref[1, 2]
    ls_copy = remote(lossx_ref.at[core], lossx_ref.at[core], ls_send, ls_recv, partner)
    ls_copy.start()

    def grad_second(b, carry):
        grad_block(1, b)
        return carry

    lax.fori_loop(0, SIDE, grad_second, 0)
    rs_start(1, 0)
    ls_copy.wait_recv()
    loss_ref[...] = jnp.broadcast_to(jnp.sum(lossx_ref[0] + lossx_ref[1]) * INV, (8, LANES))

    def flip(k, carry):
        kz, ky = lax.div(lax.rem(k, 8), 2), lax.rem(k, 2) * 2
        xs = x_ref[lax.div(k, 8), kz, pl.ds(ky, 2)].reshape(LANES, HID)
        w_ref[1, :, pl.ds(pl.multiple_of(k * LANES, LANES), LANES)] = xs.T
        return carry

    lax.fori_loop(0, 2 * 1024 // LANES, flip, 0)

    def area(k):
        return buf_ref.at[k // 2, :, pl.ds((k % 2) * 512, 512)]

    def head_copy(j, slot):
        return remote(buf_ref.at[0, :, pl.ds(pl.multiple_of(slot * 512, 512), 512)], hrecv_hbm.at[j],
                      hd_send.at[slot], hd_recv.at[j], partner)

    def head_load(j, slot):
        return pltpu.make_async_copy(hrecv_hbm.at[j], buf_ref.at[1, :, pl.ds(pl.multiple_of(slot * 512, 512), 512)],
                                     h_sem.at[slot])

    def head_dot(h, j):
        return jnp.dot(w_ref[1], g_ref[h, :, pl.ds(pl.multiple_of(j * 512, 512), 512)],
                       preferred_element_type=F32)

    def theirs(j, carry):
        slot = lax.rem(j, 2)

        @pl.when(j >= 2)
        def _():
            head_copy(j - 2, slot).wait_send()

        buf_ref[0, :, pl.ds(pl.multiple_of(slot * 512, 512), 512)] = head_dot(1 - core, j)
        head_copy(j, slot).start()
        pl.when(j == 2)(functools.partial(rs_add, 0, 0))
        return carry

    lax.fori_loop(0, 4, theirs, 0)
    head_copy(2, 0).wait_send()
    head_copy(3, 1).wait_send()

    def out_copy(j):
        at = pl.ds(pl.multiple_of(j * 512, 512), 512)
        return pltpu.make_async_copy(w_ref.at[0, :, at], dhead_hbm.at[:, at], out_sem.at[j])

    def ours(j, carry):
        slot = lax.rem(j, 2)
        head_copy(j, 0).wait_recv()
        head_load(j, slot).start()
        at = pl.ds(pl.multiple_of(j * 512, 512), 512)
        buf_ref[0, :, pl.ds(pl.multiple_of(slot * 512, 512), 512)] = head_dot(core, j)
        head_load(j, slot).wait()

        def add(i, c2):
            r = pl.ds(pl.multiple_of(i * 16, 16), 16)
            w_ref[0, r, at] = (buf_ref[0, r, pl.ds(pl.multiple_of(slot * 512, 512), 512)]
                               + buf_ref[1, r, pl.ds(pl.multiple_of(slot * 512, 512), 512)]).astype(BF16)
            return c2

        lax.fori_loop(0, HID // 16, add, 0, unroll=4)
        out_copy(j).start()
        pl.when(j == 2)(functools.partial(rs_add, 1, 0))
        pl.when(j == 3)(functools.partial(rs_add, 0, 1))
        return carry

    lax.fori_loop(0, 4, ours, 0)
    rs_add(1, 1)
    rs_add(0, 2)
    rs_add(1, 2)

    for j in range(4):
        out_copy(j).wait()
    w_copy.wait_send()
    ls_copy.wait_send()
    for phase in range(3):
        for d in (1, 2, 3):
            lab_copy(phase, d).wait_send()
            for s in range(SLABS):
                st_copy(s, phase, d).wait_send()
                for c in range(3):
                    ag_copy(s, phase, c, d).wait_send()
                    rs_copy(s, phase, c, d).wait_send()


def solution(mesh):
    any_space = pl.BlockSpec(memory_space=pl.ANY)
    vmem = pl.BlockSpec(memory_space=pltpu.VMEM)
    dma = pltpu.SemaphoreType.DMA

    def local_step(hid_loc, w_loc, lab_loc):
        labels = jnp.pad(lab_loc.reshape(1, -1), ((0, 0), (0, LANES - lab_loc.shape[0])))
        flops = 3 * 2 * TOKENS * HID * HALF
        loss, d_hidden, d_head, _, _ = pl.pallas_call(
            body,
            out_shape=(
                jax.ShapeDtypeStruct((8, LANES), F32),
                jax.ShapeDtypeStruct((SLABS * ROWS, HID), BF16),
                jax.ShapeDtypeStruct((HID, HALF), BF16),
                jax.ShapeDtypeStruct((8, 1024, 1024), F32),
                jax.ShapeDtypeStruct((4, HID, 512), F32),
            ),
            in_specs=[any_space, any_space, any_space],
            out_specs=(vmem, vmem, any_space, any_space, any_space),
            scratch_shapes=[
                pltpu.VMEM((SLABS, SIDE, SIDE, SIDE, ROWS, HID), BF16),
                pltpu.VMEM((2, HID, HALF), BF16),
                pltpu.VMEM((2, 2048, HALF), BF16),
                pltpu.VMEM((SLABS, SIDE, SIDE, SIDE, ROWS, HID), F32),
                pltpu.VMEM((2, HID, 1024), F32),
                pltpu.VMEM((SLABS, 3, 3, SIDE, SIDE, ROWS, COLOUR), F32),
                pltpu.VMEM((SLABS, 3, 3, SIDE, ROWS, COLOUR), F32),
                pltpu.VMEM((SLABS, 3, 3, ROWS, COLOUR), F32),
                pltpu.VMEM((SIDE, SIDE, SIDE, 1, LANES), jnp.int32),
                pltpu.VMEM((SLABS, 64, ROWS, LANES), jnp.int32),
                pltpu.VMEM((SLABS, 1024, LANES), F32),
                pltpu.VMEM((BLOCK, LANES), F32),
                pltpu.VMEM((BLOCK, LANES), F32),
                pltpu.VMEM((BLOCK, LANES), F32),
                pltpu.VMEM((3, 8, LANES), F32),
                pltpu.VMEM((SLABS, 3, SIDE, 3, 8, LANES), F32),
                pltpu.VMEM((SLABS, 3, 8, LANES), F32),
                pltpu.VMEM((2, 8, LANES), F32),
                dma((SLABS, 3, 3, 3)), dma((SLABS, 3, 3, 3)),
                dma((3, 3)), dma((3, 3)),
                dma, dma,
                dma((SLABS, 3, 3)), dma((SLABS, 3, 3)),
                dma((SLABS, 3, 3, 3)), dma((SLABS, 3, 3, 3)),
                dma((2,)), dma((4,)),
                dma, dma,
                dma((4,)), dma((2,)), dma((2,)), dma((2,)), dma((4,)),
            ],
            compiler_params=pltpu.CompilerParams(
                collective_id=0, has_side_effects=True, vmem_limit_bytes=67043328),
            cost_estimate=pl.CostEstimate(flops=flops, bytes_accessed=100_000_000, transcendentals=TOKENS * HALF),
        )(hid_loc, w_loc, labels)
        return loss[0, :1], d_hidden, d_head

    return jax.shard_map(
        local_step,
        mesh=mesh,
        in_specs=(P(("dp", "tp"), None), P(None, "tp"), P(("dp", "tp"))),
        out_specs=(P("dp"), P(("dp", "tp"), None), P("dp", "tp")),
        check_vma=False,
    )
```

time: 551 us -> 150 us (0.27)
  waiting for transfers between devices: 203 us -> 0 us
  blocking collectives: 196 us -> 0 us
  Pallas kernels: 0 us -> 138 us
  matrix products: 87.5 us -> 0 us
  other arithmetic: 33.2 us -> 0 us
  between operations: 15.9 us -> 0.64 us
    reduce_scatter x1 -> x0, waiting for transfers between devices: 195 us -> none  [local_step(): d_hidden = lax.psum_scatter(dx_part, 'tp', scatter_dimension=0, tiled=True)]
    pallas_call x0 -> x1, Pallas kernels: none -> 138 us  [local_step(): pl.pallas_call(body, out_shape=(jax.ShapeDtypeStruct((8, LANES), F32), ja...]
    dot_general x3 -> x0, matrix products: 87.5 us -> none  [the longest x1 30.2 us: local_step(): lax.dot_general(grad_out, w_loc, (((1,), (1,)), ((), ())), preferred_elem...]
    unnamed x1 -> x0, blocking collectives: 69.6 us -> none
    psum x1 -> x0, blocking collectives: 63.2 us -> none  [local_step(): stat_sums = lax.psum(local_stats, 'tp')]
    pmax x1 -> x0, blocking collectives: 63 us -> none  [local_step(): glob_max = lax.pmax(jnp.max(logits, axis=1), 'tp')]
    convert_element_type x2 -> x0, other arithmetic: 17.4 us -> none  [the longest x1 15.8 us: local_step(): (jnp.where(is_label, prob_rows - 1.0, prob_rows) * inv_tokens).astype(jnp...]
    reduce_sum x2 -> x0, other arithmetic: 15.8 us -> none  [the longest x1 15.2 us: local_step(): jnp.sum(shifted, axis=1)]
  transfers between devices with their start and end apart: 2 -> 0, of which waited for: 2 -> 0; matrix products, arithmetic and copies ran while one was open for 7% -> 0% of each run, Pallas kernels for 0% -> 0%
where the time goes in v1:
time: 150 us; the launch traced here: 148 us
  Pallas kernels  138 us (92%)
  local copies, waits for them, and re-layouts  9.13 us (6%)
    pallas_call x1, Pallas kernels, local_step(): pl.pallas_call(body, out_shape=(jax.ShapeDtypeStruct((8, LANES), F32), ja...  138 us
    unnamed x2, local copies, waits for them, and re-layouts  6.76 us

profile of v1, /device:TPU:1, one launch (start us, length us, event | category | flops | bytes accessed | tf_op | source)
XLA Modules:
  0.0 147.6 jit_solution(3022932440860038960)
XLA Ops:
  0.6 1.2 pad.4.lab_hbm
  1.8 137.8 %shard_map.58 = (f32[8,128]{1,0:T(8,128)}, bf16[32,1152]{1,0:T(8,128)(2,1)}, bf16[1152,2048]{1,0:T(8,128)(2,1)}, f32[8,1024,1024]{2,1,0:T(8,128)}, f32[4,1152,512]{2,1,0:T(8,128)}) custom-call(bf16[32,1152]{1,0:T(8,128)(2,1)} %x_hbm.1, bf16[1152,2048]{1,0:T(8,128)(2,1)} %w_hbm.1, s32[1,128]{1,0:T(1,128)} %pad.4.lab_hbm), custom_call_target="tpu_custom_call" | custom-call | flops 57982058496 | bytes 100000000 | tf_op jit(solution)/shard_map/pallas_call | solution.py:451
  139.6 1.2 slice.3
  140.8 1.5 %copy.8 = bf16[32,1152]{1,0:T(8,128)(2,1)} copy(bf16[32,1152]{1,0:T(8,128)(2,1)} %get-tuple-element.13) | data formatting | bytes 147456
  142.3 5.2 %copy.9 = bf16[1152,2048]{1,0:T(8,128)(2,1)} copy(bf16[1152,2048]{1,0:T(8,128)(2,1)} %get-tuple-element.14) | data formatting | bytes 9437184

commit v2 on v1

--- a/solution.py
+++ b/solution.py
@@ -28,8 +28,8 @@
 def body(x_hbm, w_hbm, lab_hbm,
          loss_ref, dhid_ref, dhead_hbm, p_hbm, hrecv_hbm,
          x_ref, w_ref, g_ref, dx_ref, buf_ref, r1_ref, r2_ref, r3_ref,
-         labrow_ref, lab_ref, m_ref, s_ref, t_ref, scale_ref, srow_ref, st_ref, fin_ref, lossx_ref,
-         ag_send, ag_recv, lab_send, lab_recv, w_send, w_recv, st_send, st_recv, rs_send, rs_recv,
+         labown_ref, labrow_ref, lab_ref, m_ref, s_ref, t_ref, scale_ref, srow_ref, st_ref, fin_ref, lossx_ref,
+         ag_send, ag_recv, lab_send, lab_recv, w_send, w_recv, st_send, st_recv, rs_send, rs_recv, r1_send, r1_recv,
          hd_send, hd_recv, ls_send, ls_recv, in_sem, p_sem, g_sem, h_sem, out_sem):
     me = lax.axis_index("tp")
     core = lax.rem(me, 2)
@@ -54,17 +54,18 @@
     for s in range(SLABS):
         own.append(pltpu.make_async_copy(x_hbm.at[pl.ds(ROWS * s, ROWS)],
                                          x_ref.at[(s,) + coords], in_sem.at[s]))
-    own.append(pltpu.make_async_copy(lab_hbm, labrow_ref.at[coords], in_sem.at[2]))
+    own.append(pltpu.make_async_copy(lab_hbm, labown_ref, in_sem.at[2]))
     w_own = pltpu.make_async_copy(w_hbm, w_ref.at[core], in_sem.at[3])
     for copy in own:
         copy.start()
     w_own.start()
 
-    barrier = pltpu.get_barrier_semaphore()
-    peers = [partner] + [rank(a, d) for a in range(3) for d in (1, 2, 3)]
-    for peer in peers:
-        pl.semaphore_signal(barrier, inc=1, device_id={"tp": peer}, device_id_type=MESH)
-    pl.semaphore_wait(barrier, len(peers))
+    with jax.named_scope("meet"):
+        barrier = pltpu.get_barrier_semaphore()
+        peers = [partner] + [rank(a, d) for a in range(3) for d in (1, 2, 3)]
+        for peer in peers:
+            pl.semaphore_signal(barrier, inc=1, device_id={"tp": peer}, device_id_type=MESH)
+        pl.semaphore_wait(barrier, len(peers))
 
     def ag_copy(s, phase, c, d):
         order = ORDERS[c]
@@ -101,26 +102,26 @@
         for d in (1, 2, 3):
             lab_copy(phase, d).wait_recv()
 
-    for copy in own:
-        copy.wait()
-    lab_start(0)
-    ag_start(0, 0)
-    ag_start(1, 0)
-    w_copy = remote(w_hbm, w_ref.at[core], w_send, w_recv, partner)
-    w_copy.start()
-    lab_wait(0)
-    lab_start(1)
-    ag_wait(0, 0)
-    ag_start(0, 1)
-    ag_wait(1, 0)
-    ag_start(1, 1)
-    lab_wait(1)
-    lab_start(2)
-    ag_wait(0, 1)
-    ag_start(0, 2)
-    ag_wait(1, 1)
-    ag_start(1, 2)
-    lab_wait(2)
+    with jax.named_scope("ag"):
+        for copy in own:
+            copy.wait()
+        labrow_ref[coords + (slice(None), slice(0, SLABS * ROWS))] = labown_ref[...]
+        ag_start(0, 0)
+        w_copy = remote(w_hbm, w_ref.at[core], w_send, w_recv, partner)
+        w_copy.start()
+        lab_start(0)
+        ag_wait(0, 0)
+        ag_start(0, 1)
+        ag_start(1, 0)
+        lab_wait(0)
+        lab_start(1)
+        ag_wait(0, 1)
+        lab_wait(1)
+        lab_start(2)
+        ag_start(0, 2)
+        ag_wait(1, 0)
+        ag_start(1, 1)
+        lab_wait(2)
 
     lane16 = lax.broadcasted_iota(jnp.int32, (ROWS, LANES), 1)
     row16 = lax.broadcasted_iota(jnp.int32, (ROWS, LANES), 0)
@@ -134,12 +135,18 @@
             lab_ref[s, k] = jnp.broadcast_to(col, (ROWS, LANES)).astype(jnp.int32) - first_col - lane16
         return carry
 
-    lax.fori_loop(0, 64, spread, 0, unroll=4)
+    with jax.named_scope("spread"):
+        lax.fori_loop(0, 64, spread, 0, unroll=4)
 
     def p_copy(n, slot):
         return pltpu.make_async_copy(buf_ref.at[slot, pl.ds(0, 1024)], p_hbm.at[n], p_sem.at[slot])
 
-    def g_load(n, slot):
+    def plane(k):
+        return lax.rem(coords[0] + k + 1, SIDE)
+
+    def g_load(t):
+        slot = lax.rem(t, 2)
+        n = lax.div(t, SIDE) * SIDE + plane(lax.rem(t, SIDE))
         return pltpu.make_async_copy(p_hbm.at[n], buf_ref.at[slot, pl.ds(0, 1024)], g_sem.at[slot])
 
     def st_copy(s, axis, d):
@@ -151,8 +158,9 @@
             st_copy(s, axis, d).start()
 
     def st_merge(s, axis):
-        for d in (1, 2, 3):
-            st_copy(s, axis, d).wait_recv()
+        with jax.named_scope("st_wait"):
+            for d in (1, 2, 3):
+                st_copy(s, axis, d).wait_recv()
         top = st_ref[s, axis, 0, 0]
         for i in range(1, SIDE):
             top = jnp.maximum(top, st_ref[s, axis, i, 0])
@@ -180,10 +188,21 @@
         def _():
             p_copy(n - 2, slot).wait()
 
-        xb = x_ref[s, b].reshape(BLOCK, HID)
-        for q in range(4):
-            buf_ref[slot, pl.ds(q * BLOCK, BLOCK), :] = jnp.dot(
-                xb, w_ref[q // 2, :, (q % 2) * 1024:(q % 2 + 1) * 1024], preferred_element_type=F32)
+        with jax.named_scope("z_dot"):
+            xb = x_ref[s, b].reshape(BLOCK, HID)
+            for q in range(4):
+                buf_ref[slot, pl.ds(q * BLOCK, BLOCK), :] = jnp.dot(
+                    xb, w_ref[q // 2, :, (q % 2) * 1024:(q % 2 + 1) * 1024], preferred_element_type=F32)
+
+        @pl.when(n == 0)
+        def _():
+            ag_wait(1, 1)
+            ag_start(1, 2)
+
+        @pl.when(n == 2 * SIDE - 1)
+        def _():
+            p_copy(2 * SIDE - 2, 0).wait()
+            g_load(0).start()
 
         def rows(i, carry):
             r0 = pl.multiple_of(i * 8, 8)
@@ -207,17 +226,19 @@
             t_ref[pl.ds(r0, 8), :] = tgt[0] + tgt[1]
             return carry
 
-        lax.fori_loop(0, BLOCK // 8, rows, 0, unroll=2)
+        with jax.named_scope("z_rows"):
+            lax.fori_loop(0, BLOCK // 8, rows, 0, unroll=2)
         p_copy(n, slot).start()
-        for i in range(2):
-            m_t = m_ref[s, pl.ds(pl.multiple_of(b * BLOCK + i * LANES, LANES), LANES), :].T
-            s_t = s_ref[i * LANES:(i + 1) * LANES, :].T
-            t_t = t_ref[i * LANES:(i + 1) * LANES, :].T
-            top = jnp.max(m_t, axis=0, keepdims=True)
-            at = pl.ds(b * 2 + i, 1)
-            srow_ref[0, at, :] = top
-            srow_ref[1, at, :] = jnp.sum(s_t * jnp.exp(m_t - top), axis=0, keepdims=True)
-            srow_ref[2, at, :] = jnp.sum(t_t, axis=0, keepdims=True)
+        with jax.named_scope("z_stat"):
+            for i in range(2):
+                m_t = m_ref[s, pl.ds(pl.multiple_of(b * BLOCK + i * LANES, LANES), LANES), :].T
+                s_t = s_ref[i * LANES:(i + 1) * LANES, :].T
+                t_t = t_ref[i * LANES:(i + 1) * LANES, :].T
+                top = jnp.max(m_t, axis=0, keepdims=True)
+                at = pl.ds(b * 2 + i, 1)
+                srow_ref[0, at, :] = top
+                srow_ref[1, at, :] = jnp.sum(s_t * jnp.exp(m_t - top), axis=0, keepdims=True)
+                srow_ref[2, at, :] = jnp.sum(t_t, axis=0, keepdims=True)
 
     def st_begin(s):
         for k in range(3):
@@ -234,6 +255,29 @@
         return remote(dx_ref.at[(s,) + tuple(idx) + (slice(None), cols(c))], land.at[s, c, d - 1],
                       rs_send.at[s, phase, c, d - 1], rs_recv.at[s, phase, c, d - 1], rank(order[phase], d))
 
+    def rs_plane(s, k, c, d):
+        axis = ORDERS[c][0]
+        b = plane(k)
+        idx = [b, slice(None), slice(None)]
+        if axis:
+            idx[axis] = ring(axis, d)
+        return remote(dx_ref.at[(s,) + tuple(idx) + (slice(None), cols(c))], r1_ref.at[s, c, d - 1, b],
+                      r1_send.at[s, c, k, d - 1], r1_recv.at[s, c, k, d - 1], rank(axis, d))
+
+    def rs_line(s, k):
+        b = plane(k)
+        return remote(dx_ref.at[s, b, :, :, :, cols(2)], r1_ref.at[s, 2, k],
+                      rs_send.at[s, 0, 2, k], rs_recv.at[s, 0, 2, k], rank(0, k + 1))
+
+    def rs_first(s, k):
+        for d in (2, 1, 3):
+            for c in range(2):
+                rs_plane(s, k, c, d).start()
+
+        @pl.when(k < SIDE - 1)
+        def _():
+            rs_line(s, k).start()
+
     def rs_start(s, phase):
         for d in (2, 1, 3):
             for c in range(3):
@@ -241,8 +285,15 @@
 
     def rs_add(s, phase):
         for c in range(3):
-            for d in (1, 2, 3):
-                rs_copy(s, phase, c, d).wait_recv()
+            with jax.named_scope("rs_wait"):
+                for d in (1, 2, 3):
+                    if phase:
+                        rs_copy(s, phase, c, d).wait_recv()
+                    elif c == 2:
+                        rs_line(s, d - 1).wait_recv()
+                    else:
+                        for k in range(SIDE):
+                            rs_plane(s, k, c, d).wait_recv()
             order = ORDERS[c]
             sl = slice(c * COLOUR, (c + 1) * COLOUR)
             idx = [None] * 3
@@ -277,21 +328,24 @@
         if phase < 2:
             rs_start(s, phase + 1)
 
-    def grad_block(s, b):
+    def grad_block(s, k):
+        b = plane(k)
         n = s * SIDE + b
-        slot = lax.rem(n, 2)
-
-        @pl.when(n < 2 * SIDE - 1)
+        t = s * SIDE + k
+        slot = lax.rem(t, 2)
+
+        @pl.when(t < 2 * SIDE - 1)
         def _():
-            g_load(n + 1, 1 - slot).start()
-
-        for i in range(2):
-            at = pl.ds(b * 2 + i, 1)
-            top = jnp.broadcast_to(fin_ref[s, 0, at, :], (LANES, LANES)).T
-            inv = jnp.broadcast_to(fin_ref[s, 1, at, :], (LANES, LANES)).T
-            m = m_ref[s, pl.ds(pl.multiple_of(b * BLOCK + i * LANES, LANES), LANES), :]
-            scale_ref[i * LANES:(i + 1) * LANES, :] = jnp.exp(m - top) * inv
-        g_load(n, slot).wait()
+            g_load(t + 1).start()
+
+        with jax.named_scope("g_scale"):
+            for i in range(2):
+                at = pl.ds(b * 2 + i, 1)
+                top = jnp.broadcast_to(fin_ref[s, 0, at, :], (LANES, LANES)).T
+                inv = jnp.broadcast_to(fin_ref[s, 1, at, :], (LANES, LANES)).T
+                m = m_ref[s, pl.ds(pl.multiple_of(b * BLOCK + i * LANES, LANES), LANES), :]
+                scale_ref[i * LANES:(i + 1) * LANES, :] = jnp.exp(m - top) * inv
+        g_load(t).wait()
 
         def rows(i, carry):
             r0 = pl.multiple_of(i * ROWS, ROWS)
@@ -305,16 +359,20 @@
                 g_ref[k // 16, pl.ds(out_row, ROWS), (k % 16) * LANES:(k % 16 + 1) * LANES] = g.astype(BF16)
             return carry
 
-        lax.fori_loop(0, BLOCK // ROWS, rows, 0, unroll=2)
+        with jax.named_scope("g_rows"):
+            lax.fori_loop(0, BLOCK // ROWS, rows, 0, unroll=2)
         at = pl.ds(pl.multiple_of(n * BLOCK, BLOCK), BLOCK)
         nt = (((1,), (1,)), ((), ()))
-        dx = (lax.dot_general(g_ref[0, at, :], w_ref[0], nt, preferred_element_type=F32)
-              + lax.dot_general(g_ref[1, at, :], w_ref[1], nt, preferred_element_type=F32))
-        dx_ref[s, b] = dx.reshape(SIDE, SIDE, ROWS, HID)
-
-    w_own.wait()
-    w_copy.wait_recv()
-    ag_wait(0, 2)
+        with jax.named_scope("dx_dot"):
+            dx = (lax.dot_general(g_ref[0, at, :], w_ref[0], nt, preferred_element_type=F32)
+                  + lax.dot_general(g_ref[1, at, :], w_ref[1], nt, preferred_element_type=F32))
+            dx_ref[s, b] = dx.reshape(SIDE, SIDE, ROWS, HID)
+        rs_first(s, k)
+
+    with jax.named_scope("first_wait"):
+        w_own.wait()
+        w_copy.wait_recv()
+        ag_wait(0, 2)
 
     def logits_first(b, carry):
         logits_block(0, b)
@@ -322,7 +380,8 @@
 
     lax.fori_loop(0, SIDE, logits_first, 0)
     st_begin(0)
-    ag_wait(1, 2)
+    with jax.named_scope("second_wait"):
+        ag_wait(1, 2)
 
     def logits_second(b, carry):
         logits_block(1, b)
@@ -332,9 +391,7 @@
 
     lax.fori_loop(0, SIDE, logits_second, 0)
     st_begin(1)
-    p_copy(6, 0).wait()
     p_copy(7, 1).wait()
-    g_load(0, 0).start()
 
     def grad_first(b, carry):
         grad_block(0, b)
@@ -343,7 +400,6 @@
         return carry
 
     lax.fori_loop(0, SIDE, grad_first, 0)
-    rs_start(0, 0)
 
     lossx_ref[core] = fin_ref[0, 2] + fin_ref[1, 2]
     ls_copy = remote(lossx_ref.at[core], lossx_ref.at[core], ls_send, ls_recv, partner)
@@ -351,12 +407,12 @@
 
     def grad_second(b, carry):
         grad_block(1, b)
+        pl.when(b == 2)(functools.partial(rs_add, 0, 0))
         return carry
 
     lax.fori_loop(0, SIDE, grad_second, 0)
-    rs_start(1, 0)
     ls_copy.wait_recv()
-    loss_ref[...] = jnp.broadcast_to(jnp.sum(lossx_ref[0] + lossx_ref[1]) * INV, (8, LANES))
+    loss_ref[0] = jnp.sum(lossx_ref[0] + lossx_ref[1]) * INV
 
     def flip(k, carry):
         kz, ky = lax.div(lax.rem(k, 8), 2), lax.rem(k, 2) * 2
@@ -364,101 +420,129 @@
         w_ref[1, :, pl.ds(pl.multiple_of(k * LANES, LANES), LANES)] = xs.T
         return carry
 
-    lax.fori_loop(0, 2 * 1024 // LANES, flip, 0)
-
-    def area(k):
-        return buf_ref.at[k // 2, :, pl.ds((k % 2) * 512, 512)]
-
-    def head_copy(j, slot):
-        return remote(buf_ref.at[0, :, pl.ds(pl.multiple_of(slot * 512, 512), 512)], hrecv_hbm.at[j],
-                      hd_send.at[slot], hd_recv.at[j], partner)
-
-    def head_load(j, slot):
-        return pltpu.make_async_copy(hrecv_hbm.at[j], buf_ref.at[1, :, pl.ds(pl.multiple_of(slot * 512, 512), 512)],
-                                     h_sem.at[slot])
+    with jax.named_scope("flip"):
+        lax.fori_loop(0, 2 * 1024 // LANES, flip, 0)
+
+    def half(slot):
+        return pl.ds(pl.multiple_of(slot * 512, 512), 512)
+
+    def head_copy(j):
+        slot = lax.rem(j, 2)
+        return remote(buf_ref.at[0, :, half(slot)], hrecv_hbm.at[j], hd_send.at[slot], hd_recv.at[j], partner)
+
+    def head_load(j):
+        return pltpu.make_async_copy(hrecv_hbm.at[j], buf_ref.at[1, :, pl.ds(512, 512)], h_sem)
 
     def head_dot(h, j):
-        return jnp.dot(w_ref[1], g_ref[h, :, pl.ds(pl.multiple_of(j * 512, 512), 512)],
-                       preferred_element_type=F32)
-
-    def theirs(j, carry):
-        slot = lax.rem(j, 2)
-
-        @pl.when(j >= 2)
+        with jax.named_scope("h_dot"):
+            return jnp.dot(w_ref[1], g_ref[h, :, half(j)], preferred_element_type=F32)
+
+    def out_copy(j):
+        return pltpu.make_async_copy(w_ref.at[0, :, half(j)], dhead_hbm.at[:, half(j)], out_sem.at[j])
+
+    def theirs(j):
+        @pl.when(jnp.int32(j) >= 2)
         def _():
-            head_copy(j - 2, slot).wait_send()
-
-        buf_ref[0, :, pl.ds(pl.multiple_of(slot * 512, 512), 512)] = head_dot(1 - core, j)
-        head_copy(j, slot).start()
-        pl.when(j == 2)(functools.partial(rs_add, 0, 0))
+            head_copy(j - 2).wait_send()
+
+        buf_ref[0, :, half(lax.rem(j, 2))] = head_dot(1 - core, j)
+        head_copy(j).start()
+
+    def ours(j):
+        with jax.named_scope("h_wait"):
+            head_copy(j).wait_recv()
+        head_load(j).start()
+        buf_ref[1, :, pl.ds(0, 512)] = head_dot(core, j)
+        with jax.named_scope("h_load"):
+            head_load(j).wait()
+
+        def add(i, carry):
+            r = pl.ds(pl.multiple_of(i * 16, 16), 16)
+            w_ref[0, r, half(j)] = (buf_ref[1, r, pl.ds(0, 512)] + buf_ref[1, r, pl.ds(512, 512)]).astype(BF16)
+            return carry
+
+        with jax.named_scope("h_add"):
+            lax.fori_loop(0, HID // 16, add, 0, unroll=4)
+        out_copy(j).start()
+
+    def pair(r, carry):
+        theirs(r + 1)
+        pl.when(r == 0)(functools.partial(rs_add, 0, 1))
+        pl.when(r == 1)(functools.partial(rs_add, 0, 2))
+        ours(r)
+        pl.when(r == 0)(functools.partial(rs_add, 1, 0))
+        pl.when(r == 1)(functools.partial(rs_add, 1, 1))
         return carry
 
-    lax.fori_loop(0, 4, theirs, 0)
-    head_copy(2, 0).wait_send()
-    head_copy(3, 1).wait_send()
-
-    def out_copy(j):
-        at = pl.ds(pl.multiple_of(j * 512, 512), 512)
-        return pltpu.make_async_copy(w_ref.at[0, :, at], dhead_hbm.at[:, at], out_sem.at[j])
-
-    def ours(j, carry):
-        slot = lax.rem(j, 2)
-        head_copy(j, 0).wait_recv()
-        head_load(j, slot).start()
-        at = pl.ds(pl.multiple_of(j * 512, 512), 512)
-        buf_ref[0, :, pl.ds(pl.multiple_of(slot * 512, 512), 512)] = head_dot(core, j)
-        head_load(j, slot).wait()
-
-        def add(i, c2):
-            r = pl.ds(pl.multiple_of(i * 16, 16), 16)
-            w_ref[0, r, at] = (buf_ref[0, r, pl.ds(pl.multiple_of(slot * 512, 512), 512)]
-                               + buf_ref[1, r, pl.ds(pl.multiple_of(slot * 512, 512), 512)]).astype(BF16)
-            return c2
-
-        lax.fori_loop(0, HID // 16, add, 0, unroll=4)
-        out_copy(j).start()
-        pl.when(j == 2)(functools.partial(rs_add, 1, 0))
-        pl.when(j == 3)(functools.partial(rs_add, 0, 1))
-        return carry
-
-    lax.fori_loop(0, 4, ours, 0)
-    rs_add(1, 1)
-    rs_add(0, 2)
+    theirs(0)
+    lax.fori_loop(0, 3, pair, 0)
     rs_add(1, 2)
-
-    for j in range(4):
-        out_copy(j).wait()
-    w_copy.wait_send()
-    ls_copy.wait_send()
-    for phase in range(3):
-        for d in (1, 2, 3):
-            lab_copy(phase, d).wait_send()
-            for s in range(SLABS):
-                st_copy(s, phase, d).wait_send()
-                for c in range(3):
-                    ag_copy(s, phase, c, d).wait_send()
-                    rs_copy(s, phase, c, d).wait_send()
+    ours(3)
+    head_copy(2).wait_send()
+    head_copy(3).wait_send()
+
+    with jax.named_scope("tail"):
+        for j in range(4):
+            out_copy(j).wait()
+        w_copy.wait_send()
+        ls_copy.wait_send()
+        for phase in range(3):
+            for d in (1, 2, 3):
+                lab_copy(phase, d).wait_send()
+                for s in range(SLABS):
+                    st_copy(s, phase, d).wait_send()
+                    for c in range(3):
+                        ag_copy(s, phase, c, d).wait_send()
+                        if phase:
+                            rs_copy(s, phase, c, d).wait_send()
+        for s in range(SLABS):
+            for d in (1, 2, 3):
+                rs_line(s, d - 1).wait_send()
+                for k in range(SIDE):
+                    for c in range(2):
+                        rs_plane(s, k, c, d).wait_send()
+
+
+PIECES = 8
+
+
+def hand_out(loss_in, dhid_in, dhead_in, loss_out, dhid_out, dhead_out, dhid_v, dhead_v, in_sem, out_sem):
+    ways = [(dhid_in, dhid_v, dhid_out)]
+    for i in range(PIECES):
+        at = pl.ds(i * (HID // PIECES), HID // PIECES)
+        ways.append((dhead_in.at[at], dhead_v.at[at], dhead_out.at[at]))
+    ins = [pltpu.make_async_copy(a, v, in_sem.at[i]) for i, (a, v, _) in enumerate(ways)]
+    outs = [pltpu.make_async_copy(v, o, out_sem.at[i]) for i, (_, v, o) in enumerate(ways)]
+    for copy in ins:
+        copy.start()
+    loss_out[0] = loss_in[0]
+    for here, there in zip(ins, outs):
+        here.wait()
+        there.start()
+    for copy in outs:
+        copy.wait()
 
 
 def solution(mesh):
     any_space = pl.BlockSpec(memory_space=pl.ANY)
     vmem = pl.BlockSpec(memory_space=pltpu.VMEM)
+    smem = pl.BlockSpec(memory_space=pltpu.SMEM)
     dma = pltpu.SemaphoreType.DMA
 
     def local_step(hid_loc, w_loc, lab_loc):
-        labels = jnp.pad(lab_loc.reshape(1, -1), ((0, 0), (0, LANES - lab_loc.shape[0])))
+        labels = lab_loc.reshape(1, -1)
         flops = 3 * 2 * TOKENS * HID * HALF
         loss, d_hidden, d_head, _, _ = pl.pallas_call(
             body,
             out_shape=(
-                jax.ShapeDtypeStruct((8, LANES), F32),
+                jax.ShapeDtypeStruct((1,), F32),
                 jax.ShapeDtypeStruct((SLABS * ROWS, HID), BF16),
                 jax.ShapeDtypeStruct((HID, HALF), BF16),
                 jax.ShapeDtypeStruct((8, 1024, 1024), F32),
                 jax.ShapeDtypeStruct((4, HID, 512), F32),
             ),
             in_specs=[any_space, any_space, any_space],
-            out_specs=(vmem, vmem, any_space, any_space, any_space),
+            out_specs=(smem, vmem, any_space, any_space, any_space),
             scratch_shapes=[
                 pltpu.VMEM((SLABS, SIDE, SIDE, SIDE, ROWS, HID), BF16),
                 pltpu.VMEM((2, HID, HALF), BF16),
@@ -468,6 +552,7 @@
                 pltpu.VMEM((SLABS, 3, 3, SIDE, SIDE, ROWS, COLOUR), F32),
                 pltpu.VMEM((SLABS, 3, 3, SIDE, ROWS, COLOUR), F32),
                 pltpu.VMEM((SLABS, 3, 3, ROWS, COLOUR), F32),
+                pltpu.VMEM((1, SLABS * ROWS), jnp.int32),
                 pltpu.VMEM((SIDE, SIDE, SIDE, 1, LANES), jnp.int32),
                 pltpu.VMEM((SLABS, 64, ROWS, LANES), jnp.int32),
                 pltpu.VMEM((SLABS, 1024, LANES), F32),
@@ -482,16 +567,30 @@
                 dma((3, 3)), dma((3, 3)),
                 dma, dma,
                 dma((SLABS, 3, 3)), dma((SLABS, 3, 3)),
-                dma((SLABS, 3, 3, 3)), dma((SLABS, 3, 3, 3)),
+                dma((SLABS, 3, 3, 3)), dma((SLABS, 3, 3, 3)), dma((SLABS, 2, SIDE, 3)), dma((SLABS, 2, SIDE, 3)),
                 dma((2,)), dma((4,)),
                 dma, dma,
-                dma((4,)), dma((2,)), dma((2,)), dma((2,)), dma((4,)),
+                dma((4,)), dma((2,)), dma((2,)), dma, dma((4,)),
             ],
             compiler_params=pltpu.CompilerParams(
                 collective_id=0, has_side_effects=True, vmem_limit_bytes=67043328),
             cost_estimate=pl.CostEstimate(flops=flops, bytes_accessed=100_000_000, transcendentals=TOKENS * HALF),
         )(hid_loc, w_loc, labels)
-        return loss[0, :1], d_hidden, d_head
+        return pl.pallas_call(
+            hand_out,
+            out_shape=(
+                jax.ShapeDtypeStruct((1,), F32),
+                jax.ShapeDtypeStruct((SLABS * ROWS, HID), BF16),
+                jax.ShapeDtypeStruct((HID, HALF), BF16),
+            ),
+            in_specs=[smem, any_space, any_space],
+            out_specs=(smem, any_space, any_space),
+            scratch_shapes=[
+                pltpu.VMEM((SLABS * ROWS, HID), BF16),
+                pltpu.VMEM((HID, HALF), BF16),
+                dma((PIECES + 1,)), dma((PIECES + 1,)),
+            ],
+        )(loss, d_hidden, d_head)
 
     return jax.shard_map(
         local_step,

time: 150 us -> 144 us (0.960); the launches traced: 148 us -> 144 us
  local copies, waits for them, and re-layouts: 9.13 us -> 0 us
  Pallas kernels: 138 us -> 143 us
    unnamed x2 -> x0, local copies, waits for them, and re-layouts: 6.76 us -> none
    pallas_call x1 -> x2, Pallas kernels: 138 us -> 143 us  [the longest x1 138 us: local_step(): pl.pallas_call(body, out_shape=(jax.ShapeDtypeStruct((1,), F32), jax.Shap...]
where the time goes in v2:
time: 144 us
  Pallas kernels  143 us (99%)
    pallas_call x1, Pallas kernels, local_step(): pl.pallas_call(body, out_shape=(jax.ShapeDtypeStruct((1,), F32), jax.Shap...  138 us
    pallas_call x1, Pallas kernels, local_step(): pl.pallas_call(hand_out, out_shape=(jax.ShapeDtypeStruct((1,), F32), jax....  5.34 us

profile of v2, /device:TPU:1, one launch (start us, length us, event | category | flops | bytes accessed | tf_op | source)
XLA Modules:
  0.0 144.1 jit_solution(1345066103272584913)
XLA Ops:
  0.6 137.9 %shard_map.58 = (f32[1]{0:T(128)}, bf16[32,1152]{1,0:T(8,128)(2,1)}, bf16[1152,2048]{1,0:T(8,128)(2,1)}, f32[8,1024,1024]{2,1,0:T(8,128)}, f32[4,1152,512]{2,1,0:T(8,128)}) custom-call(bf16[32,1152]{1,0:T(8,128)(2,1)} %x_hbm.1, bf16[1152,2048]{1,0:T(8,128)(2,1)} %w_hbm.1, s32[1,32]{1,0:T(1,128)} %bitcast.1), custom_call_target="tpu_custom_call" | custom-call | flops 57982058496 | bytes 100000000 | tf_op jit(solution)/shard_map/pallas_call | solution.py:535
  138.6 5.3 %shard_map.59 = (f32[1]{0:T(128)}, bf16[32,1152]{1,0:T(8,128)(2,1)}, bf16[1152,2048]{1,0:T(8,128)(2,1)}) custom-call(f32[1]{0:T(128)} %get-tuple-element.6.loss_in, bf16[32,1152]{1,0:T(8,128)(2,1)} %get-tuple-element.7.dhid_in, bf16[1152,2048]{1,0:T(8,128)(2,1)} %get-tuple-element.8.dhead_in), custom_call_target="tpu_custom_call" | custom-call | tf_op jit(solution)/shard_map/pallas_call | solution.py:579

commit v3 on v2

--- a/solution.py
+++ b/solution.py
@@ -29,7 +29,7 @@
          loss_ref, dhid_ref, dhead_hbm, p_hbm, hrecv_hbm,
          x_ref, w_ref, g_ref, dx_ref, buf_ref, r1_ref, r2_ref, r3_ref,
          labown_ref, labrow_ref, lab_ref, m_ref, s_ref, t_ref, scale_ref, srow_ref, st_ref, fin_ref, lossx_ref,
-         ag_send, ag_recv, lab_send, lab_recv, w_send, w_recv, st_send, st_recv, rs_send, rs_recv, r1_send, r1_recv,
+         ag_send, ag_recv, lab_send, lab_recv, w_send, w_recv, st_send, st_recv, rs_send, rs_recv,
          hd_send, hd_recv, ls_send, ls_recv, in_sem, p_sem, g_sem, h_sem, out_sem):
     me = lax.axis_index("tp")
     core = lax.rem(me, 2)
@@ -73,7 +73,7 @@
         for a in order[:phase]:
             idx[a] = slice(None)
         view = x_ref.at[(s,) + tuple(idx) + (slice(None), cols(c))]
-        return remote(view, view, ag_send.at[s, phase, c, d - 1], ag_recv.at[s, phase, c, d - 1],
+        return remote(view, view, ag_send.at[s, phase], ag_recv.at[s, phase],
                       rank(order[phase], d))
 
     def ag_start(s, phase):
@@ -81,10 +81,12 @@
             for c in range(3):
                 ag_copy(s, phase, c, d).start()
 
+    def ag_all(s, phase):
+        view = (x_ref.at[s, 0, 0, pl.ds(0, 3)], x_ref.at[s, 0, pl.ds(0, 3)], x_ref.at[s, pl.ds(0, 3)])[phase]
+        return remote(view, view, ag_send.at[s, phase], ag_recv.at[s, phase], partner)
+
     def ag_wait(s, phase):
-        for d in (1, 2, 3):
-            for c in range(3):
-                ag_copy(s, phase, c, d).wait_recv()
+        ag_all(s, phase).wait_recv()
 
     def lab_copy(phase, d):
         order = ORDERS[0]
@@ -92,15 +94,18 @@
         for a in order[:phase]:
             idx[a] = slice(None)
         view = labrow_ref.at[tuple(idx)]
-        return remote(view, view, lab_send.at[phase, d - 1], lab_recv.at[phase, d - 1], rank(order[phase], d))
+        return remote(view, view, lab_send.at[phase], lab_recv.at[phase], rank(order[phase], d))
 
     def lab_start(phase):
         for d in (1, 2, 3):
             lab_copy(phase, d).start()
 
+    def lab_all(phase):
+        view = (labrow_ref.at[0, 0, pl.ds(0, 3)], labrow_ref.at[0, pl.ds(0, 3)], labrow_ref.at[pl.ds(0, 3)])[phase]
+        return remote(view, view, lab_send.at[phase], lab_recv.at[phase], partner)
+
     def lab_wait(phase):
-        for d in (1, 2, 3):
-            lab_copy(phase, d).wait_recv()
+        lab_all(phase).wait_recv()
 
     with jax.named_scope("ag"):
         for copy in own:
@@ -151,7 +156,11 @@
 
     def st_copy(s, axis, d):
         view = st_ref.at[s, axis, coords[axis]]
-        return remote(view, view, st_send.at[s, axis, d - 1], st_recv.at[s, axis, d - 1], rank(axis, d))
+        return remote(view, view, st_send.at[s, axis], st_recv.at[s, axis], rank(axis, d))
+
+    def st_all(s, axis):
+        view = st_ref.at[s, axis, pl.ds(0, 3)]
+        return remote(view, view, st_send.at[s, axis], st_recv.at[s, axis], partner)
 
     def st_start(s, axis):
         for d in (2, 1, 3):
@@ -159,8 +168,7 @@
 
     def st_merge(s, axis):
         with jax.named_scope("st_wait"):
-            for d in (1, 2, 3):
-                st_copy(s, axis, d).wait_recv()
+            st_all(s, axis).wait_recv()
         top = st_ref[s, axis, 0, 0]
         for i in range(1, SIDE):
             top = jnp.maximum(top, st_ref[s, axis, i, 0])
@@ -253,7 +261,7 @@
         idx[order[phase]] = ring(order[phase], d)
         land = (r1_ref, r2_ref, r3_ref)[phase]
         return remote(dx_ref.at[(s,) + tuple(idx) + (slice(None), cols(c))], land.at[s, c, d - 1],
-                      rs_send.at[s, phase, c, d - 1], rs_recv.at[s, phase, c, d - 1], rank(order[phase], d))
+                      rs_send.at[s, phase], rs_recv.at[s, phase], rank(order[phase], d))
 
     def rs_plane(s, k, c, d):
         axis = ORDERS[c][0]
@@ -262,12 +270,12 @@
         if axis:
             idx[axis] = ring(axis, d)
         return remote(dx_ref.at[(s,) + tuple(idx) + (slice(None), cols(c))], r1_ref.at[s, c, d - 1, b],
-                      r1_send.at[s, c, k, d - 1], r1_recv.at[s, c, k, d - 1], rank(axis, d))
+                      rs_send.at[s, 0], rs_recv.at[s, 0], rank(axis, d))
 
     def rs_line(s, k):
         b = plane(k)
         return remote(dx_ref.at[s, b, :, :, :, cols(2)], r1_ref.at[s, 2, k],
-                      rs_send.at[s, 0, 2, k], rs_recv.at[s, 0, 2, k], rank(0, k + 1))
+                      rs_send.at[s, 0], rs_recv.at[s, 0], rank(0, k + 1))
 
     def rs_first(s, k):
         for d in (2, 1, 3):
@@ -278,22 +286,19 @@
         def _():
             rs_line(s, k).start()
 
+    def rs_all(s, phase):
+        view = (r1_ref.at[s], r2_ref.at[s], r3_ref.at[s])[phase]
+        return remote(view, view, rs_send.at[s, phase], rs_recv.at[s, phase], partner)
+
     def rs_start(s, phase):
         for d in (2, 1, 3):
             for c in range(3):
                 rs_copy(s, phase, c, d).start()
 
     def rs_add(s, phase):
+        with jax.named_scope("rs_wait"):
+            rs_all(s, phase).wait_recv()
         for c in range(3):
-            with jax.named_scope("rs_wait"):
-                for d in (1, 2, 3):
-                    if phase:
-                        rs_copy(s, phase, c, d).wait_recv()
-                    elif c == 2:
-                        rs_line(s, d - 1).wait_recv()
-                    else:
-                        for k in range(SIDE):
-                            rs_plane(s, k, c, d).wait_recv()
             order = ORDERS[c]
             sl = slice(c * COLOUR, (c + 1) * COLOUR)
             idx = [None] * 3
@@ -334,10 +339,6 @@
         t = s * SIDE + k
         slot = lax.rem(t, 2)
 
-        @pl.when(t < 2 * SIDE - 1)
-        def _():
-            g_load(t + 1).start()
-
         with jax.named_scope("g_scale"):
             for i in range(2):
                 at = pl.ds(b * 2 + i, 1)
@@ -361,12 +362,23 @@
 
         with jax.named_scope("g_rows"):
             lax.fori_loop(0, BLOCK // ROWS, rows, 0, unroll=2)
+
+        @pl.when(t == 0)
+        def _():
+            p_copy(2 * SIDE - 1, 1).wait()
+            st_merge(1, 0)
+
+        @pl.when(t < 2 * SIDE - 1)
+        def _():
+            g_load(t + 1).start()
+
         at = pl.ds(pl.multiple_of(n * BLOCK, BLOCK), BLOCK)
         nt = (((1,), (1,)), ((), ()))
         with jax.named_scope("dx_dot"):
             dx = (lax.dot_general(g_ref[0, at, :], w_ref[0], nt, preferred_element_type=F32)
                   + lax.dot_general(g_ref[1, at, :], w_ref[1], nt, preferred_element_type=F32))
             dx_ref[s, b] = dx.reshape(SIDE, SIDE, ROWS, HID)
+        pl.when(t == 0)(functools.partial(st_merge, 1, 1))
         rs_first(s, k)
 
     with jax.named_scope("first_wait"):
@@ -391,12 +403,10 @@
 
     lax.fori_loop(0, SIDE, logits_second, 0)
     st_begin(1)
-    p_copy(7, 1).wait()
 
     def grad_first(b, carry):
         grad_block(0, b)
-        for axis in range(3):
-            pl.when(b == axis)(functools.partial(st_merge, 1, axis))
+        pl.when(b == 2)(functools.partial(st_merge, 1, 2))
         return carry
 
     lax.fori_loop(0, SIDE, grad_first, 0)
@@ -467,17 +477,17 @@
 
     def pair(r, carry):
         theirs(r + 1)
-        pl.when(r == 0)(functools.partial(rs_add, 0, 1))
-        pl.when(r == 1)(functools.partial(rs_add, 0, 2))
+        pl.when(r == 1)(functools.partial(rs_add, 0, 1))
+        pl.when(r == 2)(functools.partial(rs_add, 1, 1))
         ours(r)
         pl.when(r == 0)(functools.partial(rs_add, 1, 0))
-        pl.when(r == 1)(functools.partial(rs_add, 1, 1))
+        pl.when(r == 2)(functools.partial(rs_add, 0, 2))
         return carry
 
     theirs(0)
     lax.fori_loop(0, 3, pair, 0)
+    ours(3)
     rs_add(1, 2)
-    ours(3)
     head_copy(2).wait_send()
     head_copy(3).wait_send()
 
@@ -487,20 +497,11 @@
         w_copy.wait_send()
         ls_copy.wait_send()
         for phase in range(3):
-            for d in (1, 2, 3):
-                lab_copy(phase, d).wait_send()
-                for s in range(SLABS):
-                    st_copy(s, phase, d).wait_send()
-                    for c in range(3):
-                        ag_copy(s, phase, c, d).wait_send()
-                        if phase:
-                            rs_copy(s, phase, c, d).wait_send()
-        for s in range(SLABS):
-            for d in (1, 2, 3):
-                rs_line(s, d - 1).wait_send()
-                for k in range(SIDE):
-                    for c in range(2):
-                        rs_plane(s, k, c, d).wait_send()
+            lab_all(phase).wait_send()
+            for s in range(SLABS):
+                st_all(s, phase).wait_send()
+                ag_all(s, phase).wait_send()
+                rs_all(s, phase).wait_send()
 
 
 PIECES = 8
@@ -563,11 +564,11 @@
                 pltpu.VMEM((SLABS, 3, SIDE, 3, 8, LANES), F32),
                 pltpu.VMEM((SLABS, 3, 8, LANES), F32),
                 pltpu.VMEM((2, 8, LANES), F32),
-                dma((SLABS, 3, 3, 3)), dma((SLABS, 3, 3, 3)),
-                dma((3, 3)), dma((3, 3)),
+                dma((SLABS, 3)), dma((SLABS, 3)),
+                dma((3,)), dma((3,)),
                 dma, dma,
-                dma((SLABS, 3, 3)), dma((SLABS, 3, 3)),
-                dma((SLABS, 3, 3, 3)), dma((SLABS, 3, 3, 3)), dma((SLABS, 2, SIDE, 3)), dma((SLABS, 2, SIDE, 3)),
+                dma((SLABS, 3)), dma((SLABS, 3)),
+                dma((SLABS, 3)), dma((SLABS, 3)),
                 dma((2,)), dma((4,)),
                 dma, dma,
                 dma((4,)), dma((2,)), dma((2,)), dma, dma((4,)),

time: 144 us -> 137 us (0.951)
  Pallas kernels: 143 us -> 136 us
    pallas_call x1, Pallas kernels: 138 us -> 130 us  [local_step(): pl.pallas_call(body, out_shape=(jax.ShapeDtypeStruct((1,), F32), jax.Shap...]
where the time goes in v3:
time: 137 us; the launch traced here: 136 us
  Pallas kernels  136 us (99%)
    pallas_call x1, Pallas kernels, local_step(): pl.pallas_call(body, out_shape=(jax.ShapeDtypeStruct((1,), F32), jax.Shap...  130 us
    pallas_call x1, Pallas kernels, local_step(): pl.pallas_call(hand_out, out_shape=(jax.ShapeDtypeStruct((1,), F32), jax....  5.34 us

profile of v3, /device:TPU:1, one launch (start us, length us, event | category | flops | bytes accessed | tf_op | source)
XLA Modules:
  0.0 136.4 jit_solution(14044146902009963521)
XLA Ops:
  0.6 130.3 %shard_map.58 = (f32[1]{0:T(128)}, bf16[32,1152]{1,0:T(8,128)(2,1)}, bf16[1152,2048]{1,0:T(8,128)(2,1)}, f32[8,1024,1024]{2,1,0:T(8,128)}, f32[4,1152,512]{2,1,0:T(8,128)}) custom-call(bf16[32,1152]{1,0:T(8,128)(2,1)} %x_hbm.1, bf16[1152,2048]{1,0:T(8,128)(2,1)} %w_hbm.1, s32[1,32]{1,0:T(1,128)} %bitcast.1), custom_call_target="tpu_custom_call" | custom-call | flops 57982058496 | bytes 100000000 | tf_op jit(solution)/shard_map/pallas_call | solution.py:536
  130.9 5.3 %shard_map.59 = (f32[1]{0:T(128)}, bf16[32,1152]{1,0:T(8,128)(2,1)}, bf16[1152,2048]{1,0:T(8,128)(2,1)}) custom-call(f32[1]{0:T(128)} %get-tuple-element.6.loss_in, bf16[32,1152]{1,0:T(8,128)(2,1)} %get-tuple-element.7.dhid_in, bf16[1152,2048]{1,0:T(8,128)(2,1)} %get-tuple-element.8.dhead_in), custom_call_target="tpu_custom_call" | custom-call | tf_op jit(solution)/shard_map/pallas_call | solution.py:580

commit v4 on v3

v4 whole, which is shorter than its diff:
```python
import functools

import jax
import jax.numpy as jnp
from jax import lax
from jax.experimental import pallas as pl
from jax.experimental.pallas import tpu as pltpu
from jax.sharding import PartitionSpec as P

MESH = pl.DeviceIdType.MESH
F32 = jnp.float32
BF16 = jnp.bfloat16

SIDE = 4
STRIDES = (32, 8, 2)
ORDERS = ((2, 1, 0), (1, 0, 2), (0, 2, 1))
SLABS = 2
ROWS = 16
BLOCK = 256
HID = 1152
COLOUR = HID // 3
HEAD_ROWS = 384
WIDE = 1024
HEAD = 512
SUB = 8
ALL = slice(None)
FAR = (2, 1, 3)
NEXT = (1, 2, 3)
THREE = pl.ds(0, 3)
FULL = pl.ds(0, WIDE)
HALF = 2048
TOKENS = 4096
INV = 1.0 / TOKENS
LANES = 128


def body(x_hbm, w_hbm, lab_hbm,
         loss_ref, dhid_ref, dhead_hbm, p_hbm, hrecv_hbm,
         x_ref, w_ref, ga_ref, gb_ref, dx_ref, bufa_ref, bufb_ref, r1_ref, r2_ref, r3_ref,
         labown_ref, labrow_ref, lab_ref, m_ref, mt_ref, s_ref, t_ref, srow_ref, st_ref, fin_ref, lossx_ref,
         ag_send, ag_recv, a3_send, a3_recv, lab_send, lab_recv, w_send, w_recv, st_send, st_recv, rs_send, rs_recv,
         hd_send, hd_recv, ls_send, ls_recv, in_sem, p_sem, g_sem, h_sem, out_sem):
    me = lax.axis_index("tp")
    core = lax.rem(me, 2)
    chip = lax.div(me, 2)
    coords = (lax.div(chip, ROWS), lax.rem(lax.div(chip, 4), 4), lax.rem(chip, 4))
    partner = me + 1 - 2 * core

    def ring(axis, d):
        return lax.rem(coords[axis] + d, SIDE)

    def rank(axis, d):
        return me + (ring(axis, d) - coords[axis]) * STRIDES[axis]

    def remote(src, dst, send, recv, target):
        return pltpu.make_async_remote_copy(src_ref=src, dst_ref=dst, send_sem=send, recv_sem=recv,
                                            device_id={"tp": target}, device_id_type=MESH)

    def cols(c):
        return pl.ds(COLOUR * c, COLOUR)

    own = []
    for s in range(SLABS):
        own.append(pltpu.make_async_copy(x_hbm.at[pl.ds(ROWS * s, ROWS)],
                                         x_ref.at[(s,) + coords], in_sem.at[s]))
    own.append(pltpu.make_async_copy(lab_hbm, labown_ref, in_sem.at[2]))
    w_own = pltpu.make_async_copy(w_hbm, w_ref.at[core], in_sem.at[3])
    for copy in own:
        copy.start()
    w_own.start()

    with jax.named_scope("meet"):
        barrier = pltpu.get_barrier_semaphore()
        peers = [partner] + [rank(a, d) for a in range(3) for d in NEXT]
        for peer in peers:
            pl.semaphore_signal(barrier, inc=1, device_id={"tp": peer}, device_id_type=MESH)
        pl.semaphore_wait(barrier, len(peers))

    def ag_copy(s, phase, c, d):
        order = ORDERS[c]
        idx = list(coords)
        for a in order[:phase]:
            idx[a] = ALL
        view = x_ref.at[(s,) + tuple(idx) + (ALL, cols(c))]
        return remote(view, view, ag_send.at[s, phase], ag_recv.at[s, phase],
                      rank(order[phase], d))

    def ag_start(s, phase):
        for d in FAR:
            for c in range(3):
                ag_copy(s, phase, c, d).start()

    def ag_all(s, phase):
        view = (x_ref.at[s, 0, 0, THREE], x_ref.at[s, 0, THREE], x_ref.at[s, THREE])[phase]
        return remote(view, view, ag_send.at[s, phase], ag_recv.at[s, phase], partner)

    def ag_wait(s, phase):
        ag_all(s, phase).wait_recv()

    def near(k):
        return lax.rem(coords[0] + k, SIDE)

    def ag_plane(k, c, d):
        axis = ORDERS[c][2]
        idx = [near(k), ALL, ALL]
        idx[axis] = coords[axis]
        view = x_ref.at[(0,) + tuple(idx) + (ALL, cols(c))]
        return remote(view, view, a3_send.at[0], a3_recv.at[0, k], rank(axis, d))

    def ag_line(k):
        view = x_ref.at[0, coords[0], :, :, :, cols(0)]
        return remote(view, view, a3_send.at[1], a3_recv.at[1, k], rank(0, SIDE - k))

    def ag_near(k):
        for d in FAR:
            for c in (1, 2):
                ag_plane(k, c, d).start()
        if k:
            ag_line(k).start()

    def ag_near_wait(k):
        view = x_ref.at[0, pl.ds(0, 2), 0]
        remote(view, view, a3_send.at[0], a3_recv.at[0, k], partner).wait_recv()

    def ag_line_wait(k):
        view = x_ref.at[0, 0, :, :, :, cols(0)]
        remote(view, view, a3_send.at[1], a3_recv.at[1, k], partner).wait_recv()

    def ag_near_sent():
        view = x_ref.at[0, pl.ds(0, 2)]
        remote(view, view, a3_send.at[0], a3_recv.at[0, 0], partner).wait_send()
        view = x_ref.at[0, THREE, :, :, :, cols(0)]
        remote(view, view, a3_send.at[1], a3_recv.at[1, 0], partner).wait_send()

    def lab_copy(phase, d):
        order = ORDERS[0]
        idx = list(coords)
        for a in order[:phase]:
            idx[a] = ALL
        view = labrow_ref.at[tuple(idx)]
        return remote(view, view, lab_send.at[phase], lab_recv.at[phase], rank(order[phase], d))

    def lab_start(phase):
        for d in NEXT:
            lab_copy(phase, d).start()

    def lab_all(phase):
        view = (labrow_ref.at[0, 0, THREE], labrow_ref.at[0, THREE], labrow_ref.at[THREE])[phase]
        return remote(view, view, lab_send.at[phase], lab_recv.at[phase], partner)

    def lab_wait(phase):
        lab_all(phase).wait_recv()

    with jax.named_scope("ag"):
        for copy in own:
            copy.wait()
        labrow_ref[coords + (ALL, slice(0, SLABS * ROWS))] = labown_ref[...]
        ag_start(0, 0)
        w_copy = remote(w_hbm, w_ref.at[core], w_send, w_recv, partner)
        w_copy.start()
        lab_start(0)
        ag_wait(0, 0)
        ag_start(0, 1)
        ag_start(1, 0)
        lab_wait(0)
        lab_start(1)
        ag_wait(0, 1)
        lab_wait(1)
        lab_start(2)
        ag_near(0)
        ag_near(1)
        ag_wait(1, 0)
        ag_start(1, 1)
        ag_near(2)
        ag_near(3)
        lab_wait(2)

    lane16 = lax.broadcasted_iota(jnp.int32, (ROWS, LANES), 1)
    row16 = lax.broadcasted_iota(jnp.int32, (ROWS, LANES), 0)
    first_col = chip * (2 * HALF)

    def spread(k, carry):
        kz, ky, kx = lax.div(k, ROWS), lax.rem(lax.div(k, 4), 4), lax.rem(k, 4)
        row = jnp.broadcast_to(labrow_ref[kz, ky, kx], (ROWS, LANES)).astype(F32)
        for s in range(SLABS):
            col = jnp.sum(jnp.where(lane16 == row16 + ROWS * s, row, 0.0), axis=1, keepdims=True)
            lab_ref[s, k] = jnp.broadcast_to(col, (ROWS, LANES)).astype(jnp.int32) - first_col - lane16
        return carry

    with jax.named_scope("spread"):
        lax.fori_loop(0, 64, spread, 0, unroll=4)

    bufs = (bufa_ref, bufb_ref)

    def p_copy(n, slot, q, r, rows):
        at = pl.ds(pl.multiple_of(q * BLOCK + r, SUB), rows)
        return pltpu.make_async_copy(bufs[slot].at[at], p_hbm.at[n, at], p_sem.at[slot])

    def p_start(n, slot, r, rows):
        for q in range(4):
            p_copy(n, slot, q, r, rows).start()

    def p_wait(n, slot):
        at = FULL
        pltpu.make_async_copy(bufs[slot].at[at], p_hbm.at[n], p_sem.at[slot]).wait()

    def plane(k):
        return lax.rem(coords[0] + k + 1, SIDE)

    def place(t):
        return lax.div(t, SIDE), plane(lax.rem(t, SIDE))

    def g_load(t, slot):
        s, b = place(t)
        return pltpu.make_async_copy(p_hbm.at[s * SIDE + b], bufs[slot].at[FULL], g_sem.at[slot])

    def p_ahead():
        n = plane(0)

        def line(j, carry):
            q, y, x = lax.div(j, ROWS), lax.rem(lax.div(j, 4), 4), lax.rem(j, 4)
            pltpu.make_async_copy(p_hbm.at[n, pl.ds(pl.multiple_of(j * ROWS, ROWS), ROWS)],
                                  dx_ref.at[1, q, y, x, :, FULL], g_sem.at[2]).start()
            return carry

        lax.fori_loop(0, 64, line, 0)

    def p_there():
        at = FULL
        pltpu.make_async_copy(p_hbm.at[0], bufa_ref.at[at], g_sem.at[2]).wait()

    def st_copy(s, axis, d):
        view = st_ref.at[s, axis, coords[axis]]
        return remote(view, view, st_send.at[s, axis], st_recv.at[s, axis], rank(axis, d))

    def st_all(s, axis):
        view = st_ref.at[s, axis, THREE]
        return remote(view, view, st_send.at[s, axis], st_recv.at[s, axis], partner)

    def st_start(s, axis):
        for d in FAR:
            st_copy(s, axis, d).start()

    def st_merge(s, axis):
        with jax.named_scope("st_wait"):
            st_all(s, axis).wait_recv()
        top = st_ref[s, axis, 0, 0]
        for i in range(1, SIDE):
            top = jnp.maximum(top, st_ref[s, axis, i, 0])
        total = jnp.zeros_like(top)
        target = jnp.zeros_like(top)
        for i in range(SIDE):
            total += st_ref[s, axis, i, 1] * jnp.exp(st_ref[s, axis, i, 0] - top)
            target += st_ref[s, axis, i, 2]
        if axis < 2:
            here = coords[axis + 1]
            st_ref[s, axis + 1, here, 0] = top
            st_ref[s, axis + 1, here, 1] = total
            st_ref[s, axis + 1, here, 2] = target
            st_start(s, axis + 1)
        else:
            fin_ref[s, 0] = top
            fin_ref[s, 1] = INV / total
            fin_ref[s, 2] = top + jnp.log(total) - target

    def z_group(n, slot, i):
        buf = bufs[slot]
        s, b = lax.div(n, SIDE), lax.rem(n, SIDE)
        at = [pl.ds(pl.multiple_of(q * BLOCK + i * SUB, SUB), SUB) for q in range(4)]
        part, row = pl.ds(pl.multiple_of(lax.rem(i, 2) * SUB, SUB), SUB), lax.div(i, 2)
        here = pl.ds(pl.multiple_of(i * SUB, SUB), SUB)
        lab = lab_ref[s, b * ROWS + row, part, :]
        z = [buf[at[q], l * LANES:(l + 1) * LANES] for q in range(4) for l in range(SUB)]
        tops = z
        while len(tops) > 1:
            tops = [jnp.maximum(tops[k], tops[k + 1]) for k in range(0, len(tops), 2)]
        top = tops[0]
        sums = [jnp.zeros((SUB, LANES), F32) for _ in range(2)]
        tgt = [jnp.zeros((SUB, LANES), F32) for _ in range(2)]
        for k in range(32):
            p = jnp.exp(z[k] - top)
            buf[at[k // SUB], k % SUB * LANES:(k % SUB + 1) * LANES] = p
            sums[k % 2] += p
            tgt[k % 2] = jnp.where(lab == k * LANES, z[k], tgt[k % 2])
        mt_ref[here, :] = top
        s_ref[here, :] = sums[0] + sums[1]
        t_ref[here, :] = tgt[0] + tgt[1]

    def z_stat(n):
        s, b = lax.div(n, SIDE), lax.rem(n, SIDE)
        for i in range(2):
            m = mt_ref[i * LANES:(i + 1) * LANES, :]
            m_ref[s, pl.ds(pl.multiple_of(b * BLOCK + i * LANES, LANES), LANES), :] = m
            m_t = m.T
            s_t = s_ref[i * LANES:(i + 1) * LANES, :].T
            t_t = t_ref[i * LANES:(i + 1) * LANES, :].T
            top = jnp.max(m_t, axis=0, keepdims=True)
            at = pl.ds(b * 2 + i, 1)
            srow_ref[0, at, :] = top
            srow_ref[1, at, :] = jnp.sum(s_t * jnp.exp(m_t - top), axis=0, keepdims=True)
            srow_ref[2, at, :] = jnp.sum(t_t, axis=0, keepdims=True)

    def z_step(t, slot):
        s, k = lax.div(t, SIDE), lax.rem(t, SIDE)
        b = near(k)
        n = s * SIDE + b

        @pl.when(t >= 2)
        def _():
            p_wait(n, slot)

        with jax.named_scope("z_dot"):
            xb = x_ref[s, b].reshape(BLOCK, HID)
            for q in range(4):
                bufs[slot][pl.ds(q * BLOCK, BLOCK), :] = jnp.dot(
                    xb, w_ref[q // 2, :, q % 2 * WIDE:(q % 2 + 1) * WIDE], preferred_element_type=F32)
        if slot:
            @pl.when(t == 2 * SIDE - 1)
            def _():
                p_wait(n, 0)
                g_load(1, 0).start()

        def rows(i, carry):
            z_group(n, slot, i)
            return carry

        with jax.named_scope("z_rows"):
            lax.fori_loop(0, 32, rows, 0, unroll=4)
        p_start(n, slot, 0, BLOCK)
        with jax.named_scope("z_stat"):
            z_stat(n)

    def st_begin(s):
        for k in range(3):
            st_ref[s, 0, coords[0], k] = srow_ref[k]
        st_start(s, 0)

    def rs_copy(s, phase, c, d):
        order = ORDERS[c]
        idx = [ALL] * 3
        for a in order[:phase]:
            idx[a] = coords[a]
        idx[order[phase]] = ring(order[phase], d)
        land = (r1_ref, r2_ref, r3_ref)[phase]
        return remote(dx_ref.at[(s,) + tuple(idx) + (ALL, cols(c))], land.at[s, c, d - 1],
                      rs_send.at[s, phase], rs_recv.at[s, phase], rank(order[phase], d))

    def rs_plane(s, k, c, d):
        axis = ORDERS[c][0]
        b = plane(k)
        idx = [b, ALL, ALL]
        if axis:
            idx[axis] = ring(axis, d)
        return remote(dx_ref.at[(s,) + tuple(idx) + (ALL, cols(c))], r1_ref.at[s, c, d - 1, b],
                      rs_send.at[s, 0], rs_recv.at[s, 0], rank(axis, d))

    def rs_line(s, k):
        b = plane(k)
        return remote(dx_ref.at[s, b, :, :, :, cols(2)], r1_ref.at[s, 2, k],
                      rs_send.at[s, 0], rs_recv.at[s, 0], rank(0, k + 1))

    def rs_first(t):
        s, k = lax.div(t, SIDE), lax.rem(t, SIDE)
        for d in FAR:
            for c in range(2):
                rs_plane(s, k, c, d).start()

        @pl.when(k < SIDE - 1)
        def _():
            rs_line(s, k).start()

    def rs_all(s, phase):
        view = (r1_ref.at[s], r2_ref.at[s], r3_ref.at[s])[phase]
        return remote(view, view, rs_send.at[s, phase], rs_recv.at[s, phase], partner)

    def rs_start(s, phase):
        for d in FAR:
            for c in range(3):
                rs_copy(s, phase, c, d).start()

    def rs_add(s, phase):
        with jax.named_scope("rs_wait"):
            rs_all(s, phase).wait_recv()
        for c in range(3):
            order = ORDERS[c]
            sl = slice(c * COLOUR, (c + 1) * COLOUR)
            idx = [None] * 3
            for a in order[:phase + 1]:
                idx[a] = coords[a]
            free = [a for a in range(3) if idx[a] is None]
            if phase == 0:
                def add(i, carry):
                    for j in range(SIDE):
                        at = list(idx)
                        at[free[0]], at[free[1]] = i, j
                        at = (s,) + tuple(at)
                        dx_ref[at + (ALL, sl)] = (
                            (dx_ref[at + (ALL, sl)] + r1_ref[s, c, 0, i, j])
                            + (r1_ref[s, c, 1, i, j] + r1_ref[s, c, 2, i, j]))
                    return carry
                lax.fori_loop(0, SIDE, add, 0)
            elif phase == 1:
                def add(i, carry):
                    at = list(idx)
                    at[free[0]] = i
                    at = (s,) + tuple(at)
                    dx_ref[at + (ALL, sl)] = (
                        (dx_ref[at + (ALL, sl)] + r2_ref[s, c, 0, i])
                        + (r2_ref[s, c, 1, i] + r2_ref[s, c, 2, i]))
                    return carry
                lax.fori_loop(0, SIDE, add, 0)
            else:
                total = ((dx_ref[(s,) + tuple(idx) + (ALL, sl)] + r3_ref[s, c, 0])
                         + (r3_ref[s, c, 1] + r3_ref[s, c, 2]))
                dhid_ref[s * ROWS:(s + 1) * ROWS, sl] = total.astype(BF16)
        if phase < 2:
            rs_start(s, phase + 1)

    gs = (ga_ref, gb_ref)
    last = jnp.int32(2 * SIDE - 1)

    def g_scale(t):
        s, b = place(t)
        for i in range(2):
            at = pl.ds(b * 2 + i, 1)
            top = jnp.broadcast_to(fin_ref[s, 0, at, :], (LANES, LANES)).T
            inv = jnp.broadcast_to(fin_ref[s, 1, at, :], (LANES, LANES)).T
            m = m_ref[s, pl.ds(pl.multiple_of(b * BLOCK + i * LANES, LANES), LANES), :]
            s_ref[i * LANES:(i + 1) * LANES, :] = jnp.exp(m - top) * inv

    def g_group(t, slot, i, ahead=True):
        s, b = place(t)
        at = [pl.ds(pl.multiple_of(q * BLOCK + i * ROWS, ROWS), ROWS) for q in range(4)]
        here = pl.ds(pl.multiple_of(i * ROWS, ROWS), ROWS)
        lab = lab_ref[s, b * ROWS + i]
        scale = s_ref[here, :]
        out = pl.ds(pl.multiple_of(lax.div(t, 2) * BLOCK + i * ROWS, ROWS), ROWS)
        for k in range(32):
            lanes = slice(k % SUB * LANES, (k % SUB + 1) * LANES)
            if ahead:
                p = bufs[1 - slot][at[k // SUB], lanes]
            else:
                p = dx_ref[1, k // SUB, lax.div(i, 4), lax.rem(i, 4), :, lanes]
            g = p * scale - jnp.where(lab == k * LANES, INV, 0.0)
            gs[slot][k // ROWS, out, k % ROWS * LANES:(k % ROWS + 1) * LANES] = g.astype(BF16)

    nt = (((1,), (1,)), ((), ()))

    def dx_dot(t, slot, h):
        at = pl.ds(pl.multiple_of(lax.div(t, 2) * BLOCK, BLOCK), BLOCK)
        return lax.dot_general(gs[slot][h, at, :], w_ref[h], nt, preferred_element_type=F32)

    def dx_store(t, dx):
        s, b = place(t)
        dx_ref[s, b] = dx.reshape(SIDE, SIDE, ROWS, HID)

    def g_step(t, slot):
        with jax.named_scope("g_load"):
            g_load(t, 1 - slot).wait()

        @pl.when(t < 2 * SIDE - 1)
        def _():
            pl.when(t == 1)(functools.partial(p_wait, 0, 1))
            g_load(t + 1, slot).start()

        with jax.named_scope("g_step"):
            g_scale(t)
            for i in range(ROWS):
                g_group(t, slot, i)
            dx_store(t - 1, dx_dot(t - 1, 1 - slot, 0) + dx_dot(t - 1, 1 - slot, 1))

    with jax.named_scope("first_wait"):
        w_own.wait()
        w_copy.wait_recv()
        ag_near_wait(0)

    def z_pair(i, carry):
        t = 2 * i

        with jax.named_scope("z_wait"):
            @pl.when(i == 1)
            def _():
                ag_near_wait(2)
                ag_line_wait(2)

            pl.when(i == 2)(functools.partial(ag_wait, 1, 2))
        z_step(t, 0)
        with jax.named_scope("z_wait"):
            @pl.when(i == 0)
            def _():
                ag_wait(1, 1)
                ag_start(1, 2)
                ag_near_wait(1)
                ag_line_wait(1)

            @pl.when(i == 1)
            def _():
                ag_near_wait(3)
                ag_line_wait(3)

            pl.when(i == 2)(functools.partial(st_merge, 0, 0))
            pl.when(i == 3)(functools.partial(st_merge, 0, 2))
        z_step(t + 1, 1)

        @pl.when(i == 1)
        def _():
            st_begin(0)
            p_ahead()

        pl.when(i == 2)(functools.partial(st_merge, 0, 1))
        return carry

    lax.fori_loop(0, SIDE, z_pair, 0)
    st_begin(1)

    def g_first(i, carry):
        g_group(jnp.int32(0), 0, i, False)
        return carry

    with jax.named_scope("g_first"):
        g_scale(jnp.int32(0))
        p_there()
        lax.fori_loop(0, ROWS, g_first, 0, unroll=2)

    def g_pair(i, carry):
        t = 2 * i + 1
        g_step(t, 1)
        pl.when(i == 0)(functools.partial(st_merge, 1, 0))
        pl.when(i == 1)(functools.partial(st_merge, 1, 2))
        rs_first(t - 1)

        @pl.when(i < SIDE - 1)
        def _():
            g_step(t + 1, 0)
            pl.when(i == 0)(functools.partial(st_merge, 1, 1))
            rs_first(t)

        return carry

    lax.fori_loop(0, SIDE, g_pair, 0)
    with jax.named_scope("dx_last"):
        dx_store(last, dx_dot(last, 1, 0) + dx_dot(last, 1, 1))
    rs_first(last)
    rs_add(0, 0)

    lossx_ref[core] = fin_ref[0, 2] + fin_ref[1, 2]
    ls_copy = remote(lossx_ref.at[core], lossx_ref.at[core], ls_send, ls_recv, partner)
    ls_copy.start()

    ls_copy.wait_recv()
    loss_ref[0] = jnp.sum(lossx_ref[0] + lossx_ref[1]) * INV

    def flip(j, carry):
        t, part = lax.div(j, 2), lax.rem(j, 2)
        s, b = place(t)
        xs = x_ref[s, b, pl.ds(part * 2, 2)].reshape(LANES, HID)
        at = lax.rem(t, 2) * WIDE + lax.div(t, 2) * BLOCK + part * LANES
        w_ref[1, :, pl.ds(pl.multiple_of(at, LANES), LANES)] = xs.T
        return carry

    with jax.named_scope("flip"):
        lax.fori_loop(0, 2 * WIDE // LANES, flip, 0)

    def half(slot):
        return pl.ds(pl.multiple_of(slot * HEAD, HEAD), HEAD)

    def head_copy(j):
        slot = lax.rem(j, 2)
        return remote(bufa_ref.at[:, half(slot)], hrecv_hbm.at[j], hd_send.at[slot], hd_recv.at[j], partner)

    def head_load(j):
        return pltpu.make_async_copy(hrecv_hbm.at[j], bufb_ref.at[:, pl.ds(HEAD, HEAD)], h_sem)

    def head_dot(h, j, buf, at):
        with jax.named_scope("h_dot"):
            for r in range(0, HID, HEAD_ROWS):
                r = pl.ds(r, HEAD_ROWS)
                buf[r, at] = (jnp.dot(w_ref[1, r, :WIDE], ga_ref[h, :, half(j)], preferred_element_type=F32)
                              + jnp.dot(w_ref[1, r, WIDE:], gb_ref[h, :, half(j)], preferred_element_type=F32))

    def out_copy(j):
        return pltpu.make_async_copy(w_ref.at[0, :, half(j)], dhead_hbm.at[:, half(j)], out_sem.at[j])

    def theirs(j):
        @pl.when(jnp.int32(j) >= 2)
        def _():
            head_copy(j - 2).wait_send()

        head_dot(1 - core, j, bufa_ref, half(lax.rem(j, 2)))
        head_copy(j).start()

    def ours(j):
        head_dot(core, j, bufb_ref, pl.ds(0, HEAD))

    def fetch(j):
        with jax.named_scope("h_wait"):
            head_copy(j).wait_recv()
        head_load(j).start()

    def finish(j):
        with jax.named_scope("h_load"):
            head_load(j).wait()

        def add(i, carry):
            r = pl.ds(pl.multiple_of(i * ROWS, ROWS), ROWS)
            w_ref[0, r, half(j)] = (bufb_ref[r, pl.ds(0, HEAD)] + bufb_ref[r, pl.ds(HEAD, HEAD)]).astype(BF16)
            return carry

        with jax.named_scope("h_add"):
            lax.fori_loop(0, HID // ROWS, add, 0, unroll=SIDE)
        out_copy(j).start()

    def pair(r, carry):
        theirs(r + 1)

        @pl.when(r > 0)
        def _():
            finish(r - 1)

        pl.when(r == 1)(functools.partial(rs_add, 0, 1))
        ours(r)
        fetch(r)
        pl.when(r == 0)(functools.partial(rs_add, 1, 0))
        pl.when(r == 2)(functools.partial(rs_add, 1, 1))
        return carry

    theirs(0)
    lax.fori_loop(0, 3, pair, 0)
    rs_add(0, 2)
    finish(2)
    fetch(3)
    ours(3)
    finish(3)
    rs_add(1, 2)
    head_copy(2).wait_send()
    head_copy(3).wait_send()

    with jax.named_scope("tail"):
        for j in range(4):
            out_copy(j).wait()
        w_copy.wait_send()
        ls_copy.wait_send()
        ag_near_sent()
        for phase in range(3):
            lab_all(phase).wait_send()
            for s in range(SLABS):
                st_all(s, phase).wait_send()
                if s or phase < 2:
                    ag_all(s, phase).wait_send()
                rs_all(s, phase).wait_send()


PIECES = 8


def hand_out(loss_in, dhid_in, dhead_in, loss_out, dhid_out, dhead_out, dhid_v, dhead_v, in_sem, out_sem):
    ways = [(dhid_in, dhid_v, dhid_out)]
    for i in range(PIECES):
        at = pl.ds(i * (HID // PIECES), HID // PIECES)
        ways.append((dhead_in.at[at], dhead_v.at[at], dhead_out.at[at]))
    ins = [pltpu.make_async_copy(a, v, in_sem.at[i]) for i, (a, v, _) in enumerate(ways)]
    outs = [pltpu.make_async_copy(v, o, out_sem.at[i]) for i, (_, v, o) in enumerate(ways)]
    for copy in ins:
        copy.start()
    loss_out[0] = loss_in[0]
    for here, there in zip(ins, outs):
        here.wait()
        there.start()
    for copy in outs:
        copy.wait()


def solution(mesh):
    any_space = pl.BlockSpec(memory_space=pl.ANY)
    vmem = pl.BlockSpec(memory_space=pltpu.VMEM)
    smem = pl.BlockSpec(memory_space=pltpu.SMEM)
    dma = pltpu.SemaphoreType.DMA

    def local_step(hid_loc, w_loc, lab_loc):
        labels = lab_loc.reshape(1, -1)
        flops = 3 * 2 * TOKENS * HID * HALF
        loss, d_hidden, d_head, _, _ = pl.pallas_call(
            body,
            out_shape=(
                jax.ShapeDtypeStruct((1,), F32),
                jax.ShapeDtypeStruct((SLABS * ROWS, HID), BF16),
                jax.ShapeDtypeStruct((HID, HALF), BF16),
                jax.ShapeDtypeStruct((SUB, WIDE, WIDE), F32),
                jax.ShapeDtypeStruct((4, HID, HEAD), F32),
            ),
            in_specs=[any_space, any_space, any_space],
            out_specs=(smem, vmem, any_space, any_space, any_space),
            scratch_shapes=[
                pltpu.VMEM((SLABS, SIDE, SIDE, SIDE, ROWS, HID), BF16),
                pltpu.VMEM((2, HID, HALF), BF16),
                pltpu.VMEM((2, WIDE, HALF), BF16),
                pltpu.VMEM((2, WIDE, HALF), BF16),
                pltpu.VMEM((SLABS, SIDE, SIDE, SIDE, ROWS, HID), F32),
                pltpu.VMEM((HID, WIDE), F32),
                pltpu.VMEM((HID, WIDE), F32),
                pltpu.VMEM((SLABS, 3, 3, SIDE, SIDE, ROWS, COLOUR), F32),
                pltpu.VMEM((SLABS, 3, 3, SIDE, ROWS, COLOUR), F32),
                pltpu.VMEM((SLABS, 3, 3, ROWS, COLOUR), F32),
                pltpu.VMEM((1, SLABS * ROWS), jnp.int32),
                pltpu.VMEM((SIDE, SIDE, SIDE, 1, LANES), jnp.int32),
                pltpu.VMEM((SLABS, 64, ROWS, LANES), jnp.int32),
                pltpu.VMEM((SLABS, WIDE, LANES), F32),
                pltpu.VMEM((BLOCK, LANES), F32),
                pltpu.VMEM((BLOCK, LANES), F32),
                pltpu.VMEM((BLOCK, LANES), F32),
                pltpu.VMEM((3, SUB, LANES), F32),
                pltpu.VMEM((SLABS, 3, SIDE, 3, SUB, LANES), F32),
                pltpu.VMEM((SLABS, 3, SUB, LANES), F32),
                pltpu.VMEM((2, SUB, LANES), F32),
                dma((SLABS, 3)), dma((SLABS, 3)), dma((2,)), dma((2, SIDE)),
                dma((3,)), dma((3,)),
                dma, dma,
                dma((SLABS, 3)), dma((SLABS, 3)),
                dma((SLABS, 3)), dma((SLABS, 3)),
                dma((2,)), dma((4,)),
                dma, dma,
                dma((4,)), dma((2,)), dma((3,)), dma, dma((4,)),
            ],
            compiler_params=pltpu.CompilerParams(
                collective_id=0, has_side_effects=True, vmem_limit_bytes=67043328),
            cost_estimate=pl.CostEstimate(flops=flops, bytes_accessed=100_000_000, transcendentals=TOKENS * HALF),
        )(hid_loc, w_loc, labels)
        return pl.pallas_call(
            hand_out,
            out_shape=(
                jax.ShapeDtypeStruct((1,), F32),
                jax.ShapeDtypeStruct((SLABS * ROWS, HID), BF16),
                jax.ShapeDtypeStruct((HID, HALF), BF16),
            ),
            in_specs=[smem, any_space, any_space],
            out_specs=(smem, any_space, any_space),
            scratch_shapes=[
                pltpu.VMEM((SLABS * ROWS, HID), BF16),
                pltpu.VMEM((HID, HALF), BF16),
                dma((PIECES + 1,)), dma((PIECES + 1,)),
            ],
        )(loss, d_hidden, d_head)

    return jax.shard_map(
        local_step,
        mesh=mesh,
        in_specs=(P(("dp", "tp"), None), P(None, "tp"), P(("dp", "tp"))),
        out_specs=(P("dp"), P(("dp", "tp"), None), P("dp", "tp")),
        check_vma=False,
    )
```

time: 137 us -> 138 us (level)
  no operation moved by 1% of the time
where the time goes in v4:
time: 138 us; the launch traced here: 137 us
  Pallas kernels  136 us (99%)
    pallas_call x1, Pallas kernels, local_step(): pl.pallas_call(body, out_shape=(jax.ShapeDtypeStruct((1,), F32), jax.Shap...  131 us
    pallas_call x1, Pallas kernels, local_step(): pl.pallas_call(hand_out, out_shape=(jax.ShapeDtypeStruct((1,), F32), jax....  5.34 us

profile of v4, /device:TPU:1, one launch (start us, length us, event | category | flops | bytes accessed | tf_op | source)
XLA Modules:
  0.0 137.1 jit_solution(4658438340936283960)
XLA Ops:
  0.6 131.0 %shard_map.58 = (f32[1]{0:T(128)}, bf16[32,1152]{1,0:T(8,128)(2,1)}, bf16[1152,2048]{1,0:T(8,128)(2,1)}, f32[8,1024,1024]{2,1,0:T(8,128)}, f32[4,1152,512]{2,1,0:T(8,128)}) custom-call(bf16[32,1152]{1,0:T(8,128)(2,1)} %x_hbm.1, bf16[1152,2048]{1,0:T(8,128)(2,1)} %w_hbm.1, s32[1,32]{1,0:T(1,128)} %bitcast.1), custom_call_target="tpu_custom_call" | custom-call | flops 57982058496 | bytes 100000000 | tf_op jit(solution)/shard_map/pallas_call | solution.py:682
  131.6 5.3 %shard_map.59 = (f32[1]{0:T(128)}, bf16[32,1152]{1,0:T(8,128)(2,1)}, bf16[1152,2048]{1,0:T(8,128)(2,1)}) custom-call(f32[1]{0:T(128)} %get-tuple-element.6.loss_in, bf16[32,1152]{1,0:T(8,128)(2,1)} %get-tuple-element.7.dhid_in, bf16[1152,2048]{1,0:T(8,128)(2,1)} %get-tuple-element.8.dhead_in), custom_call_target="tpu_custom_call" | custom-call | tf_op jit(solution)/shard_map/pallas_call | solution.py:728

commit v5 on v4

--- a/solution.py
+++ b/solution.py
@@ -37,7 +37,7 @@
 def body(x_hbm, w_hbm, lab_hbm,
          loss_ref, dhid_ref, dhead_hbm, p_hbm, hrecv_hbm,
          x_ref, w_ref, ga_ref, gb_ref, dx_ref, bufa_ref, bufb_ref, r1_ref, r2_ref, r3_ref,
-         labown_ref, labrow_ref, lab_ref, m_ref, mt_ref, s_ref, t_ref, srow_ref, st_ref, fin_ref, lossx_ref,
+         labown_ref, labrow_ref, lab_ref, m_ref, mt_ref, s_ref, t_ref, scale_ref, srow_ref, st_ref, fin_ref, lossx_ref,
          ag_send, ag_recv, a3_send, a3_recv, lab_send, lab_recv, w_send, w_recv, st_send, st_recv, rs_send, rs_recv,
          hd_send, hd_recv, ls_send, ls_recv, in_sem, p_sem, g_sem, h_sem, out_sem):
     me = lax.axis_index("tp")
@@ -426,14 +426,14 @@
             top = jnp.broadcast_to(fin_ref[s, 0, at, :], (LANES, LANES)).T
             inv = jnp.broadcast_to(fin_ref[s, 1, at, :], (LANES, LANES)).T
             m = m_ref[s, pl.ds(pl.multiple_of(b * BLOCK + i * LANES, LANES), LANES), :]
-            s_ref[i * LANES:(i + 1) * LANES, :] = jnp.exp(m - top) * inv
+            scale_ref[i * LANES:(i + 1) * LANES, :] = jnp.exp(m - top) * inv
 
     def g_group(t, slot, i, ahead=True):
         s, b = place(t)
         at = [pl.ds(pl.multiple_of(q * BLOCK + i * ROWS, ROWS), ROWS) for q in range(4)]
         here = pl.ds(pl.multiple_of(i * ROWS, ROWS), ROWS)
         lab = lab_ref[s, b * ROWS + i]
-        scale = s_ref[here, :]
+        scale = scale_ref[here, :]
         out = pl.ds(pl.multiple_of(lax.div(t, 2) * BLOCK + i * ROWS, ROWS), ROWS)
         for k in range(32):
             lanes = slice(k % SUB * LANES, (k % SUB + 1) * LANES)
@@ -465,9 +465,16 @@
 
         with jax.named_scope("g_step"):
             g_scale(t)
-            for i in range(ROWS):
-                g_group(t, slot, i)
-            dx_store(t - 1, dx_dot(t - 1, 1 - slot, 0) + dx_dot(t - 1, 1 - slot, 1))
+            sb, bb = place(t - 1)
+
+            def part(h, carry):
+                dx = dx_dot(t - 1, 1 - slot, h).reshape(SIDE, SIDE, ROWS, HID)
+                for i in range(SUB):
+                    g_group(t, slot, h * SUB + i)
+                dx_ref[sb, bb] = dx + jnp.where(h == 0, 0.0, dx_ref[sb, bb])
+                return carry
+
+            lax.fori_loop(0, 2, part, 0)
 
     with jax.named_scope("first_wait"):
         w_own.wait()
@@ -705,6 +712,7 @@
                 pltpu.VMEM((SIDE, SIDE, SIDE, 1, LANES), jnp.int32),
                 pltpu.VMEM((SLABS, 64, ROWS, LANES), jnp.int32),
                 pltpu.VMEM((SLABS, WIDE, LANES), F32),
+                pltpu.VMEM((BLOCK, LANES), F32),
                 pltpu.VMEM((BLOCK, LANES), F32),
                 pltpu.VMEM((BLOCK, LANES), F32),
                 pltpu.VMEM((BLOCK, LANES), F32),

time: 138 us -> 130 us (0.942)
  Pallas kernels: 136 us -> 129 us
    pallas_call x1, Pallas kernels: 131 us -> 124 us  [local_step(): pl.pallas_call(body, out_shape=(jax.ShapeDtypeStruct((1,), F32), jax.Shap...]
where the time goes in v5:
time: 130 us
  Pallas kernels  129 us (99%)
    pallas_call x1, Pallas kernels, local_step(): pl.pallas_call(body, out_shape=(jax.ShapeDtypeStruct((1,), F32), jax.Shap...  124 us
    pallas_call x1, Pallas kernels, local_step(): pl.pallas_call(hand_out, out_shape=(jax.ShapeDtypeStruct((1,), F32), jax....  5.34 us

profile of v5, /device:TPU:1, one launch (start us, length us, event | category | flops | bytes accessed | tf_op | source)
XLA Modules:
  0.0 129.7 jit_solution(14974956198613454622)
XLA Ops:
  0.6 123.6 %shard_map.58 = (f32[1]{0:T(128)}, bf16[32,1152]{1,0:T(8,128)(2,1)}, bf16[1152,2048]{1,0:T(8,128)(2,1)}, f32[8,1024,1024]{2,1,0:T(8,128)}, f32[4,1152,512]{2,1,0:T(8,128)}) custom-call(bf16[32,1152]{1,0:T(8,128)(2,1)} %x_hbm.1, bf16[1152,2048]{1,0:T(8,128)(2,1)} %w_hbm.1, s32[1,32]{1,0:T(1,128)} %bitcast.1), custom_call_target="tpu_custom_call" | custom-call | flops 57982058496 | bytes 100000000 | tf_op jit(solution)/shard_map/pallas_call | solution.py:689
  124.2 5.3 %shard_map.59 = (f32[1]{0:T(128)}, bf16[32,1152]{1,0:T(8,128)(2,1)}, bf16[1152,2048]{1,0:T(8,128)(2,1)}) custom-call(f32[1]{0:T(128)} %get-tuple-element.6.loss_in, bf16[32,1152]{1,0:T(8,128)(2,1)} %get-tuple-element.7.dhid_in, bf16[1152,2048]{1,0:T(8,128)(2,1)} %get-tuple-element.8.dhead_in), custom_call_target="tpu_custom_call" | custom-call | tf_op jit(solution)/shard_map/pallas_call | solution.py:736
